TPU v7x, 32 devices: a whole 2x2x4 slice. The times are simulated.
32 devices in a mesh: rows: 8 (over z, x), cols: 4 (over y, core).
Axes of the slice: x: 2, y: 2, z: 4, core: 2. Of those that a mesh axis runs over, the one named last changes fastest.
Arguments:
- left_features: bfloat16 [2, 96, 512, 256], P(None, 'rows', 'cols'), may hold values from -6 to 6
- right_features: bfloat16 [2, 96, 512, 256], P(None, 'rows', 'cols'), may hold values from -6 to 6
- conv_weight: bfloat16 [3, 3, 256, 256], replicated, may hold values from -0.125 to 0.125
- conv_bias: float32 [256], replicated, may hold values from -3 to 3
Outputs:
- pyramid_out: float32 [2, 96, 512, 480], P(None, 'rows', 'cols')
All inputs are finite; a program needn't handle non-finite values.
Results may differ from a plain program's by a relative error of at most 0.0012.
Values may be sent and summed in bfloat16 or wider, within the bound.
No kernel may reach another device: no remote copies, remote signals or barrier semaphores. Data moves between devices by JAX's collectives and lax.ppermute only.
A program may use at most 64 MiB of HBM per device.

v0:
```python
import math

import jax
import jax.numpy as jnp
from jax import lax
from jax.sharding import PartitionSpec as P

DISP = 256
LEVELS = 4


def padded_2(cells, sides, width):
    for axis, dim in sides:
        count = lax.axis_size(axis)
        ends = count - 1
        head = lax.slice_in_dim(cells, 0, width, axis=dim)
        tail = lax.slice_in_dim(cells, cells.shape[dim] - width, cells.shape[dim], axis=dim)
        cells = jnp.concatenate(
            [
                lax.ppermute(tail, axis, [(i, (i + 1) % count) for i in range(ends)]),
                cells,
                lax.ppermute(head, axis, [((i + 1) % count, i) for i in range(ends)]),
            ],
            axis=dim,
        )
    return cells


def shifted(value, axis, steps):
    count = lax.axis_size(axis)
    leading, last = (max(0, -steps), min(count, count - steps))
    return lax.ppermute(value, axis, [(source, source + steps) for source in range(leading, last)])


def encode(padded, conv_weight, conv_bias):
    batch = padded.shape[0]
    height = padded.shape[1] - 2
    breadth = padded.shape[2] - 2
    channels = padded.shape[3]
    total = jnp.zeros((batch * height * breadth, channels), jnp.float32)
    for row_tap in range(3):
        for col_tap in range(3):
            window = padded[:, row_tap : row_tap + height, col_tap : col_tap + breadth].reshape(
                -1, channels
            )
            total = total + jnp.dot(
                window, conv_weight[row_tap, col_tap], preferred_element_type=jnp.float32
            )
    centre = padded[:, 1:-1, 1:-1].reshape(-1, channels).astype(jnp.float32)
    encoded = centre + jax.nn.relu(total + conv_bias)
    return encoded.astype(jnp.bfloat16).reshape(batch, height, breadth, channels)


def pyramid(scores, span_count, level_count, channels):
    queries = scores.shape[-2]
    across = scores.shape[-1]
    leading = scores.shape[:-2]
    skewed = scores[..., 1:].reshape(leading + (-1,))
    skewed = jnp.pad(skewed, [(0, 0)] * len(leading) + [(0, queries)])
    skewed = skewed.reshape(leading + (queries, across))[..., :span_count][..., ::-1]
    volume = skewed * (1.0 / math.sqrt(channels))
    levels = [volume]
    for level in range(1, level_count):
        pooled = volume.reshape(leading + (queries, span_count >> level, 1 << level)).mean(axis=-1)
        levels.append(pooled)
    return jnp.concatenate(levels, axis=-1)


def shards(left_features, right_features, conv_weight, conv_bias):
    batch, height, breadth, channels = left_features.shape
    left_pad, right_pad = (
        padded_2(left_features, (("rows", 1), ("cols", 2)), 1),
        padded_2(right_features, (("rows", 1), ("cols", 2)), 1),
    )
    left_out = encode(left_pad, conv_weight, conv_bias)
    right_out = encode(right_pad, conv_weight, conv_bias)
    pieces = []
    for offset in range(DISP // breadth, 0, -1):
        pieces.append(shifted(right_out, "cols", offset))
    pieces.append(right_out)
    window = jnp.concatenate(pieces, axis=2)
    rows_total = batch * height
    scores = jnp.einsum(
        "rxc,ryc->rxy",
        left_out.reshape(rows_total, breadth, channels),
        window.reshape(rows_total, DISP + breadth, channels),
        preferred_element_type=jnp.float32,
    )
    return pyramid(scores, DISP, LEVELS, channels).reshape(batch, height, breadth, -1)


def solution(mesh):
    return jax.shard_map(
        shards,
        mesh=mesh,
        in_specs=(P(None, "rows", "cols", None), P(None, "rows", "cols", None), P(), P()),
        out_specs=P(None, "rows", "cols", None),
        check_vma=False,
    )
```

profile of v0, /device:TPU:25, one launch (start us, length us, event | category | flops | bytes accessed | tf_op | source)
XLA Modules:
  0.0 127.9 jit_solution(5578612117687081469)
XLA Ops:
  1.0 3.1 %collective-permute-start = (bf16[2,1,128,256]{3,2,1,0:T(8,128)(2,1)S(1)}, bf16[2,1,128,256]{3,2,1,0:T(8,128)(2,1)S(1)}, u32[]{:S(2)}, u32[]{:S(2)}) collective-permute-start(bf16[2,1,128,256]{3,2,1,0:T(8,128)(2,1)S(1)} %get-tuple-element.36), channel_id=1, source_target_pairs={{0,4},{4,8},{8,12},{12,16},{16,20},{20,24},{24,28},{1,5},{5,9},{9,... | collective-permute-start | bytes 393224 | tf_op jit(solution)/shard_map/ppermute | solution.py:20
  4.1 3.1 %collective-permute-start.1 = (bf16[2,1,128,256]{3,2,1,0:T(8,128)(2,1)S(1)}, bf16[2,1,128,256]{3,2,1,0:T(8,128)(2,1)S(1)}, u32[]{:S(2)}, u32[]{:S(2)}) collective-permute-start(bf16[2,1,128,256]{3,2,1,0:T(8,128)(2,1)S(1)} %get-tuple-element.35), channel_id=1, source_target_pairs={{4,0},{8,4},{12,8},{16,12},{20,16},{24,20},{28,24},{5,1},{9,5},{13... | collective-permute-start | bytes 393224 | tf_op jit(solution)/shard_map/ppermute | solution.py:22
  8.2 2.2 %collective-permute-start.4 = (bf16[2,1,128,256]{3,2,1,0:T(8,128)(2,1)S(1)}, bf16[2,1,128,256]{3,2,1,0:T(8,128)(2,1)S(1)}, u32[]{:S(2)}, u32[]{:S(2)}) collective-permute-start(bf16[2,1,128,256]{3,2,1,0:T(8,128)(2,1)S(1)} %get-tuple-element.31), channel_id=1, source_target_pairs={{0,4},{4,8},{8,12},{12,16},{16,20},{20,24},{24,28},{1,5},{5,9},{9,... | collective-permute-start | bytes 393224 | tf_op jit(solution)/shard_map/ppermute | solution.py:20
  10.4 4.0 %collective-permute-start.5 = (bf16[2,1,128,256]{3,2,1,0:T(8,128)(2,1)S(1)}, bf16[2,1,128,256]{3,2,1,0:T(8,128)(2,1)S(1)}, u32[]{:S(2)}, u32[]{:S(2)}) collective-permute-start(bf16[2,1,128,256]{3,2,1,0:T(8,128)(2,1)S(1)} %get-tuple-element.30), channel_id=1, source_target_pairs={{4,0},{8,4},{12,8},{16,12},{20,16},{24,20},{28,24},{5,1},{9,5},{13... | collective-permute-start | bytes 393224 | tf_op jit(solution)/shard_map/ppermute | solution.py:22
  14.4 2.8 %pad_maximum_fusion.12 = (bf16[2,12,128,256]{3,2,1,0:T(8,128)(2,1)S(1)}, bf16[2,14,128,256]{3,2,1,0:T(8,128)(2,1)S(1)}, bf16[2,12,128,256]{3,2,1,0:T(8,128)(2,1)S(1)}) fusion(bf16[2,12,128,256]{3,2,1,0:T(8,128)(2,1)} %param.4, bf16[2,1,128,256]{3,2,1,0:T(8,128)(2,1)S(1)} %collective-permute-done, ...), kind=kLoop, calls=%fused_computation.64 | loop fusion | flops 6291456 | bytes 6553600 | tf_op jit(solution)/shard_map/concatenate | solution.py:18
  17.3 4.8 %collective-permute-start.2 = (bf16[2,14,1,256]{3,2,1,0:T(2,128)(2,1)S(1)}, bf16[2,14,1,256]{3,2,1,0:T(2,128)(2,1)S(1)}, u32[]{:S(2)}, u32[]{:S(2)}) collective-permute-start(bf16[2,14,1,256]{3,2,1,0:T(2,128)(2,1)S(1)} %get-tuple-element.25), channel_id=1, source_target_pairs={{0,1},{1,2},{2,3},{4,5},{5,6},{6,7},{8,9},{9,10},{10,11},{12,13},{... | collective-permute-start | bytes 43016 | tf_op jit(solution)/shard_map/ppermute | solution.py:20
  22.1 1.9 %collective-permute-start.3 = (bf16[2,14,1,256]{3,2,1,0:T(2,128)(2,1)S(1)}, bf16[2,14,1,256]{3,2,1,0:T(2,128)(2,1)S(1)}, u32[]{:S(2)}, u32[]{:S(2)}) collective-permute-start(bf16[2,14,1,256]{3,2,1,0:T(2,128)(2,1)S(1)} %get-tuple-element.26), channel_id=1, source_target_pairs={{1,0},{2,1},{3,2},{5,4},{6,5},{7,6},{9,8},{10,9},{11,10},{13,12},{... | collective-permute-start | bytes 43016 | tf_op jit(solution)/shard_map/ppermute | solution.py:22
  26.7 3.6 %collective-permute-start.6 = (bf16[2,14,1,256]{3,2,1,0:T(2,128)(2,1)S(1)}, bf16[2,14,1,256]{3,2,1,0:T(2,128)(2,1)S(1)}, u32[]{:S(2)}, u32[]{:S(2)}) collective-permute-start(bf16[2,14,1,256]{3,2,1,0:T(2,128)(2,1)S(1)} %get-tuple-element.20), channel_id=1, source_target_pairs={{0,1},{1,2},{2,3},{4,5},{5,6},{6,7},{8,9},{9,10},{10,11},{12,13},{... | collective-permute-start | bytes 43016 | tf_op jit(solution)/shard_map/ppermute | solution.py:20
  30.3 1.9 %collective-permute-start.7 = (bf16[2,14,1,256]{3,2,1,0:T(2,128)(2,1)S(1)}, bf16[2,14,1,256]{3,2,1,0:T(2,128)(2,1)S(1)}, u32[]{:S(2)}, u32[]{:S(2)}) collective-permute-start(bf16[2,14,1,256]{3,2,1,0:T(2,128)(2,1)S(1)} %get-tuple-element.21), channel_id=1, source_target_pairs={{1,0},{2,1},{3,2},{5,4},{6,5},{7,6},{9,8},{10,9},{11,10},{13,12},{... | collective-permute-start | bytes 43016 | tf_op jit(solution)/shard_map/ppermute | solution.py:22
  33.4 2.1 %collective-permute-done.7 = bf16[2,14,1,256]{3,2,1,0:T(2,128)(2,1)S(1)} collective-permute-done((bf16[2,14,1,256]{3,2,1,0:T(2,128)(2,1)S(1)}, bf16[2,14,1,256]{3,2,1,0:T(2,128)(2,1)S(1)}, u32[]{:S(2)}, u32[]{:S(2)}) %collective-permute-start.7) | collective-permute-done | bytes 14368 | tf_op jit(solution)/shard_map/ppermute | solution.py:22
  35.5 5.1 %pad_maximum_fusion.7 = (bf16[2,12,128,256]{3,2,1,0:T(8,128)(2,1)S(1)}, bf16[2,12,128,256]{3,2,1,0:T(8,128)(2,1)S(1)}, bf16[2,12,128,256]{3,2,1,0:T(8,128)(2,1)S...) fusion(bf16[2,14,128,256]{3,2,1,0:T(8,128)(2,1)S(1)} %constant_, ...), kind=kLoop, calls=%fused_computation.59 | loop fusion | flops 18874368 | bytes 11300864 | tf_op jit(solution)/shard_map/concatenate | solution.py:18
  45.5 1.9 %collective-permute-start.9 = (bf16[2,12,128,256]{3,2,1,0:T(8,128)(2,1)S(1)}, bf16[2,12,128,256]{3,2,1,0:T(8,128)(2,1)S(1)}, u32[]{:S(2)}, u32[]{:S(2)}) collective-permute-start(bf16[2,12,128,256]{3,2,1,0:T(8,128)(2,1)S(1)} %bitcast.120), channel_id=1, source_target_pairs={{0,1},{1,2},{2,3},{4,5},{5,6},{6,7},{8,9},{9,10},{10,11},{12,13},{... | collective-permute-start | bytes 4718600 | tf_op jit(solution)/shard_map/ppermute | solution.py:32
  47.4 1.6 %collective-permute-start.8 = (bf16[2,12,128,256]{3,2,1,0:T(8,128)(2,1)S(1)}, bf16[2,12,128,256]{3,2,1,0:T(8,128)(2,1)S(1)}, u32[]{:S(2)}, u32[]{:S(2)}) collective-permute-start(bf16[2,12,128,256]{3,2,1,0:T(8,128)(2,1)S(1)} %bitcast.121), channel_id=1, source_target_pairs={{0,2},{1,3},{4,6},{5,7},{8,10},{9,11},{12,14},{13,15},{16,18},{17,... | collective-permute-start | bytes 4718600 | tf_op jit(solution)/shard_map/ppermute | solution.py:32
  49.0 5.1 %pad_maximum_fusion.11 = (bf16[2,12,128,256]{3,2,1,0:T(8,128)(2,1)S(1)}, bf16[2,12,128,256]{3,2,1,0:T(8,128)(2,1)S(1)}, bf16[2,12,128,256]{3,2,1,0:T(8,128)(2,1)...) fusion(bf16[2,14,128,256]{3,2,1,0:T(8,128)(2,1)S(1)} %constant_, ...), kind=kLoop, calls=%fused_computation.63 | loop fusion | flops 18874368 | bytes 11300864 | tf_op jit(solution)/shard_map/concatenate | solution.py:18
  59.8 19.3 %collective-permute-done.9 = bf16[2,12,128,256]{3,2,1,0:T(8,128)(2,1)S(1)} collective-permute-done((bf16[2,12,128,256]{3,2,1,0:T(8,128)(2,1)S(1)}, bf16[2,12,128,256]{3,2,1,0:T(8,128)(2,1)S(1)}, u32[]{:S(2)}, u32[]{:S(2)}) %collective-permute-start.9) | collective-permute-done | bytes 1572896 | tf_op jit(solution)/shard_map/ppermute | solution.py:32
  79.1 19.3 %collective-permute-done.8 = bf16[2,12,128,256]{3,2,1,0:T(8,128)(2,1)S(1)} collective-permute-done((bf16[2,12,128,256]{3,2,1,0:T(8,128)(2,1)S(1)}, bf16[2,12,128,256]{3,2,1,0:T(8,128)(2,1)S(1)}, u32[]{:S(2)}, u32[]{:S(2)}) %collective-permute-start.8) | collective-permute-done | bytes 1572896 | tf_op jit(solution)/shard_map/ppermute | solution.py:32
  98.5 3.2 %fusion = f32[24,128,383]{2,1,0:T(8,128)} fusion(bf16[24,128,256]{2,1,0:T(8,128)(2,1)S(1)} %bitcast.123, bf16[24,128,256]{2,1,0:T(8,128)(2,1)S(1)} %bitcast.122, bf16[24,128,256]{2,1,0:T(8,128)(2,1)S(1)} %bitcast.124, bf16[24,128,256]{2,1,0:T(8,128)(2,1)S(1)} %bitcast.125), kind=kOutput, calls=%fused_computation.2 | convolution fusion | flops 616525824 | bytes 10997760 | tf_op jit(solution)/shard_map/rxc,ryc->rxy/dot_general | solution.py:83
  101.6 6.6 %reshape.102 = f32[24,49024]{1,0:T(8,128)} reshape(f32[24,128,383]{2,1,0:T(8,128)} %fusion) | data formatting | bytes 9412608 | tf_op jit(solution)/shard_map/reshape | solution.py:58
  108.3 2.6 %pad.4 = f32[24,49152]{1,0:T(8,128)S(1)} pad(f32[24,49024]{1,0:T(8,128)} %reshape.102, f32[]{:T(128)} %constant.6.clone.1), padding=0_0x0_128 | pad | bytes 9424900 | tf_op jit(solution)/shard_map/jit(_pad)/pad | solution.py:59
  111.7 2.0 %slice.186 = f32[24,128,256]{2,1,0:T(8,128)} slice(f32[24,128,384]{2,1,0:T(8,128)S(1)} %bitcast.109), slice={[0:24], [0:128], [0:256]} | slice | bytes 6291456 | tf_op jit(solution)/shard_map/slice | solution.py:60
  113.7 2.5 %copy.18 = f32[24,128,256]{1,0,2:T(8,128)S(1)} copy(f32[24,128,256]{2,1,0:T(8,128)} %slice.186) | data formatting | bytes 6291456
  117.2 1.9 %reverse_multiply_fusion = f32[24,128,256]{1,0,2:T(8,128)} fusion(f32[24,128,256]{1,0,2:T(8,128)S(1)} %copy.18), kind=kLoop, calls=%fused_computation.32 | loop fusion | flops 786432 | bytes 6291456 | tf_op jit(solution)/shard_map/mul | solution.py:61
  121.4 2.9 %pad_maximum_fusion = f32[24,128,480]{1,0,2:T(8,128)S(1)} fusion(f32[24,128,32]{1,0,2:T(8,128)} %copy.15, f32[24,128,64]{1,0,2:T(8,128)S(1)} %broadcast_multiply_fusion.1, f32[24,128,128]{1,0,2:T(8,128)} %broadcast_multiply_fusion, f32[24,128,256]{1,0,2:T(8,128)} %reverse_multiply_fusion), kind=kLoop, calls=%fused_computation | loop fusion | flops 4423680 | bytes 11796480 | tf_op jit(solution)/shard_map/concatenate | solution.py:66
  124.3 3.6 %copy.16 = f32[24,128,480]{1,2,0:T(8,128)} copy(f32[24,128,480]{1,0,2:T(8,128)S(1)} %pad_maximum_fusion) | data formatting | bytes 11796480 | tf_op jit(solution)/shard_map/concatenate | solution.py:66
  (50 shorter events, 20.3 us)
Async XLA Ops:
  1.0 13.4 %collective-permute-start = (bf16[2,1,128,256]{3,2,1,0:T(8,128)(2,1)S(1)}, bf16[2,1,128,256]{3,2,1,0:T(8,128)(2,1)S(1)}, u32[]{:S(2)}, u32[]{:S(2)}) collective-permute-start(bf16[2,1,128,256]{3,2,1,0:T(8,128)(2,1)S(1)} %get-tuple-element.36), channel_id=1, source_target_pairs={{0,4},{4,8},{8,12},{12,16},{16,20},{20,24},{24,28},{1,5},{5,9},{9,... | collective-permute-start | bytes 393224 | tf_op jit(solution)/shard_map/ppermute | solution.py:20
  4.1 10.3 %collective-permute-start.1 = (bf16[2,1,128,256]{3,2,1,0:T(8,128)(2,1)S(1)}, bf16[2,1,128,256]{3,2,1,0:T(8,128)(2,1)S(1)}, u32[]{:S(2)}, u32[]{:S(2)}) collective-permute-start(bf16[2,1,128,256]{3,2,1,0:T(8,128)(2,1)S(1)} %get-tuple-element.35), channel_id=1, source_target_pairs={{4,0},{8,4},{12,8},{16,12},{20,16},{24,20},{28,24},{5,1},{9,5},{13... | collective-permute-start | bytes 393224 | tf_op jit(solution)/shard_map/ppermute | solution.py:22
  8.2 17.0 %collective-permute-start.4 = (bf16[2,1,128,256]{3,2,1,0:T(8,128)(2,1)S(1)}, bf16[2,1,128,256]{3,2,1,0:T(8,128)(2,1)S(1)}, u32[]{:S(2)}, u32[]{:S(2)}) collective-permute-start(bf16[2,1,128,256]{3,2,1,0:T(8,128)(2,1)S(1)} %get-tuple-element.31), channel_id=1, source_target_pairs={{0,4},{4,8},{8,12},{12,16},{16,20},{20,24},{24,28},{1,5},{5,9},{9,... | collective-permute-start | bytes 393224 | tf_op jit(solution)/shard_map/ppermute | solution.py:20
  10.4 14.8 %collective-permute-start.5 = (bf16[2,1,128,256]{3,2,1,0:T(8,128)(2,1)S(1)}, bf16[2,1,128,256]{3,2,1,0:T(8,128)(2,1)S(1)}, u32[]{:S(2)}, u32[]{:S(2)}) collective-permute-start(bf16[2,1,128,256]{3,2,1,0:T(8,128)(2,1)S(1)} %get-tuple-element.30), channel_id=1, source_target_pairs={{4,0},{8,4},{12,8},{16,12},{20,16},{24,20},{28,24},{5,1},{9,5},{13... | collective-permute-start | bytes 393224 | tf_op jit(solution)/shard_map/ppermute | solution.py:22
  14.4 9.6 %copy-start.2 = (bf16[3,3,256,256]{3,2,1,0:T(8,128)(2,1)S(1)}, bf16[3,3,256,256]{3,2,1,0:T(8,128)(2,1)}, u32[]{:S(2)}) copy-start(bf16[3,3,256,256]{3,2,1,0:T(8,128)(2,1)} %param.6) | copy-start | bytes 3538948
  17.3 31.7 %collective-permute-start.2 = (bf16[2,14,1,256]{3,2,1,0:T(2,128)(2,1)S(1)}, bf16[2,14,1,256]{3,2,1,0:T(2,128)(2,1)S(1)}, u32[]{:S(2)}, u32[]{:S(2)}) collective-permute-start(bf16[2,14,1,256]{3,2,1,0:T(2,128)(2,1)S(1)} %get-tuple-element.25), channel_id=1, source_target_pairs={{0,1},{1,2},{2,3},{4,5},{5,6},{6,7},{8,9},{9,10},{10,11},{12,13},{... | collective-permute-start | bytes 43016 | tf_op jit(solution)/shard_map/ppermute | solution.py:20
  22.1 26.9 %collective-permute-start.3 = (bf16[2,14,1,256]{3,2,1,0:T(2,128)(2,1)S(1)}, bf16[2,14,1,256]{3,2,1,0:T(2,128)(2,1)S(1)}, u32[]{:S(2)}, u32[]{:S(2)}) collective-permute-start(bf16[2,14,1,256]{3,2,1,0:T(2,128)(2,1)S(1)} %get-tuple-element.26), channel_id=1, source_target_pairs={{1,0},{2,1},{3,2},{5,4},{6,5},{7,6},{9,8},{10,9},{11,10},{13,12},{... | collective-permute-start | bytes 43016 | tf_op jit(solution)/shard_map/ppermute | solution.py:22
  24.6 1.4 %copy-start = (bf16[2,12,128,256]{3,2,1,0:T(8,128)(2,1)S(1)}, bf16[2,12,128,256]{3,2,1,0:T(8,128)(2,1)}, u32[]{:S(2)}) copy-start(bf16[2,12,128,256]{3,2,1,0:T(8,128)(2,1)} %param.5) | copy-start | bytes 4718596
  26.7 6.7 %collective-permute-start.6 = (bf16[2,14,1,256]{3,2,1,0:T(2,128)(2,1)S(1)}, bf16[2,14,1,256]{3,2,1,0:T(2,128)(2,1)S(1)}, u32[]{:S(2)}, u32[]{:S(2)}) collective-permute-start(bf16[2,14,1,256]{3,2,1,0:T(2,128)(2,1)S(1)} %get-tuple-element.20), channel_id=1, source_target_pairs={{0,1},{1,2},{2,3},{4,5},{5,6},{6,7},{8,9},{9,10},{10,11},{12,13},{... | collective-permute-start | bytes 43016 | tf_op jit(solution)/shard_map/ppermute | solution.py:20
  30.3 5.2 %collective-permute-start.7 = (bf16[2,14,1,256]{3,2,1,0:T(2,128)(2,1)S(1)}, bf16[2,14,1,256]{3,2,1,0:T(2,128)(2,1)S(1)}, u32[]{:S(2)}, u32[]{:S(2)}) collective-permute-start(bf16[2,14,1,256]{3,2,1,0:T(2,128)(2,1)S(1)} %get-tuple-element.21), channel_id=1, source_target_pairs={{1,0},{2,1},{3,2},{5,4},{6,5},{7,6},{9,8},{10,9},{11,10},{13,12},{... | collective-permute-start | bytes 43016 | tf_op jit(solution)/shard_map/ppermute | solution.py:22
  43.6 0.7 copy-start.3
  45.5 33.6 %collective-permute-start.9 = (bf16[2,12,128,256]{3,2,1,0:T(8,128)(2,1)S(1)}, bf16[2,12,128,256]{3,2,1,0:T(8,128)(2,1)S(1)}, u32[]{:S(2)}, u32[]{:S(2)}) collective-permute-start(bf16[2,12,128,256]{3,2,1,0:T(8,128)(2,1)S(1)} %bitcast.120), channel_id=1, source_target_pairs={{0,1},{1,2},{2,3},{4,5},{5,6},{6,7},{8,9},{9,10},{10,11},{12,13},{... | collective-permute-start | bytes 4718600 | tf_op jit(solution)/shard_map/ppermute | solution.py:32
  47.4 51.0 %collective-permute-start.8 = (bf16[2,12,128,256]{3,2,1,0:T(8,128)(2,1)S(1)}, bf16[2,12,128,256]{3,2,1,0:T(8,128)(2,1)S(1)}, u32[]{:S(2)}, u32[]{:S(2)}) collective-permute-start(bf16[2,12,128,256]{3,2,1,0:T(8,128)(2,1)S(1)} %bitcast.121), channel_id=1, source_target_pairs={{0,2},{1,3},{4,6},{5,7},{8,10},{9,11},{12,14},{13,15},{16,18},{17,... | collective-permute-start | bytes 4718600 | tf_op jit(solution)/shard_map/ppermute | solution.py:32
  55.9 1.4 %copy-start.1 = (bf16[2,12,128,256]{3,2,1,0:T(8,128)(2,1)S(1)}, bf16[2,12,128,256]{3,2,1,0:T(8,128)(2,1)}, u32[]{:S(2)}) copy-start(bf16[2,12,128,256]{3,2,1,0:T(8,128)(2,1)} %param.4) | copy-start | bytes 4718596
where the time goes:
time: 129 us; the launch traced here: 128 us
  waiting for transfers between devices  40.8 us (32%)
  starting transfers between devices  28.2 us (22%)
  local copies, waits for them, and re-layouts  23 us (18%)
  other arithmetic  20.7 us (16%)
  matrix products  14.9 us (12%)
    ppermute x2, waiting for transfers between devices, shifted(): lax.ppermute(value, axis, [(source, source + steps) for source in range(l...  38.7 us
    ppermute x4, starting transfers between devices, padded_2(): lax.ppermute(tail, axis, [(i, (i + 1) % count) for i in range(ends)])  13.8 us
    concatenate x4, other arithmetic, padded_2(): jnp.concatenate([lax.ppermute(tail, axis, [(i, (i + 1) % count) for i in...  13.6 us
    dot_general x18, matrix products, encode(): jnp.dot(window, conv_weight[row_tap, col_tap], preferred_element_type=jnp...  11.7 us
    ppermute x4, starting transfers between devices, padded_2(): lax.ppermute(head, axis, [((i + 1) % count, i) for i in range(ends)])  10.9 us
    reshape x1, local copies, waits for them, and re-layouts, pyramid(): skewed = scores[..., 1:].reshape(leading + (-1,))  6.63 us
    unnamed x12, local copies, waits for them, and re-layouts  5.08 us
    concatenate x1, local copies, waits for them, and re-layouts, pyramid(): return jnp.concatenate(levels, axis=-1)  3.64 us
  transfers between devices with their start and end apart: 10, of which 3 were waited for; matrix products, arithmetic and copies ran while one was open for 21% of the time, Pallas kernels for 0%

commit v1 on v0

v1 whole, which is shorter than its diff:
```python
import math

import jax
import jax.numpy as jnp
from jax import lax
from jax.experimental import pallas as pl
from jax.experimental.pallas import tpu as pltpu
from jax.sharding import PartitionSpec as P

DISP = 256
LEVELS = 4
F32 = jnp.float32
BF16 = jnp.bfloat16
VMEM = pl.BlockSpec(memory_space=pltpu.VMEM)


def shifted(value, axis, steps):
    count = lax.axis_size(axis)
    first, last = max(0, -steps), min(count, count - steps)
    return lax.ppermute(value, axis, [(i, i + steps) for i in range(first, last)])


def iota(shape, dim):
    return lax.broadcasted_iota(jnp.int32, shape, dim)


def reversal(size):
    mirrored = iota((size, size), 0) + iota((size, size), 1) == size - 1
    return jnp.where(mirrored, 1.0, 0.0).astype(BF16)


def dot(a, b):
    return jnp.dot(a, b, preferred_element_type=F32)


def dot_t(a, b):
    return lax.dot_general(a, b, (((1,), (1,)), ((), ())), preferred_element_type=F32)


def cost(flops, nbytes):
    return pl.CostEstimate(flops=flops, bytes_accessed=nbytes, transcendentals=0)


def encode(image, side, edges, weight, bias, rows, which, mirror):
    batch, height, breadth, channels = image.shape
    count = len(rows)
    needed = sorted({r + dy for r in rows for dy in (-1, 0, 1)})
    place = {r: i for i, r in enumerate(needed)}

    def kernel(image_ref, before_ref, after_ref, *rest):
        if edges is None:
            weight_ref, bias_ref, out_ref, taps = rest
        else:
            up_ref, down_ref, weight_ref, bias_ref, out_ref, taps = rest
        spot = iota((breadth, channels), 0)
        for b in range(batch):
            for r in needed:
                if 0 <= r < height:
                    row = image_ref[b, r]
                    before = before_ref[which, b, r : r + 1, :]
                    after = after_ref[which, b, r : r + 1, :]
                else:
                    ref = up_ref if r < 0 else down_ref
                    row = ref[which, b, :breadth, :]
                    ends = ref[which, b, breadth:, :]
                    before = ends[0:1]
                    after = ends[1:2]
                wide = row.astype(F32)
                west = jnp.where(spot == 0, before.astype(F32), pltpu.roll(wide, 1, 0))
                east = jnp.where(
                    spot == breadth - 1, after.astype(F32), pltpu.roll(wide, breadth - 1, 0)
                )
                taps[place[r], :, :channels] = west.astype(BF16)
                taps[place[r], :, channels : 2 * channels] = row
                taps[place[r], :, 2 * channels :] = east.astype(BF16)
            total = None
            for dy in range(3):
                window = jnp.concatenate([taps[place[r + dy - 1]] for r in rows], axis=0)
                part = dot(window, weight_ref[dy])
                total = part if total is None else total + part
            centre = jnp.concatenate([image_ref[b, r] for r in rows], axis=0).astype(F32)
            encoded = (centre + jnp.maximum(total + bias_ref[...], 0.0)).astype(BF16)
            for i in range(count):
                value = encoded[i * breadth : (i + 1) * breadth]
                if mirror:
                    value = dot(reversal(breadth), value).astype(BF16)
                out_ref[b, i] = value

    operands = [image, side[0], side[1]] + ([] if edges is None else list(edges))
    operands += [weight.reshape(3, 3 * channels, channels), bias.reshape(1, channels)]
    return pl.pallas_call(
        kernel,
        out_shape=jax.ShapeDtypeStruct((batch, count, breadth, channels), BF16),
        in_specs=[VMEM] * len(operands),
        out_specs=VMEM,
        scratch_shapes=[pltpu.VMEM((len(needed), breadth, 3 * channels), BF16)],
        cost_estimate=cost(batch * count * breadth * channels * channels * 18, 2 * image.size),
        name="encode",
    )(*operands)


def triangle(left, right):
    batch, count, breadth, channels = left.shape

    def kernel(left_ref, right_ref, out_ref):
        near = iota((breadth, breadth), 1) > iota((breadth, breadth), 0)
        flip = reversal(breadth)
        for i in range(count):
            for b in range(0, batch, 2):
                upper = dot_t(left_ref[b, i], right_ref[b, i])
                upper = pltpu.roll(upper, 1, 1, stride=1, stride_axis=0)
                turned = dot(flip, left_ref[b + 1, i]).astype(BF16)
                lower = dot_t(turned, right_ref[b + 1, i])
                out_ref[b // 2, i] = jnp.where(near, upper, lower)

    return pl.pallas_call(
        kernel,
        out_shape=jax.ShapeDtypeStruct((batch // 2, count, breadth, breadth), F32),
        in_specs=[VMEM] * 2,
        out_specs=VMEM,
        cost_estimate=cost(2 * batch * count * breadth * breadth * channels, 4 * left.size),
        name="triangle",
    )(left, right)


def split(value):
    high = value.astype(BF16)
    return high, (value - high.astype(F32)).astype(BF16)


def volume(left, own, near, far, first, height, held):
    batch, count, breadth, channels = left.shape
    pooled = sum(DISP >> level for level in range(1, LEVELS))
    width = DISP + pooled
    scale = 1.0 / math.sqrt(channels)

    def kernel(*refs):
        left_ref, own_ref, near_ref, far_ref = refs[:4]
        out_ref = refs[-1]
        kept = iota((breadth, breadth), 1) > iota((breadth, breadth), 0)
        flip = reversal(breadth)
        source, target = iota((DISP, pooled), 0), iota((DISP, pooled), 1)
        pool = jnp.zeros((DISP, pooled), F32)
        start = 0
        for level in range(1, LEVELS):
            size = DISP >> level
            hit = (source >> level == target - start) & (target >= start) & (target < start + size)
            pool = jnp.where(hit, 1.0 / (1 << level), pool)
            start += size
        pool = pool.astype(BF16)
        for b in range(batch):
            window = jnp.concatenate([own_ref[b, 0], near_ref[b, 0]], axis=0)
            scores = dot_t(left_ref[b, 0], window)
            scores = pltpu.roll(scores, breadth + 1, 1, stride=1, stride_axis=0)
            corner = far_ref[b // 2, 0]
            if b % 2:
                high, low = split(corner)
                corner = dot(flip, high) + dot(flip, low)
                corner = pltpu.roll(corner, 1, 1, stride=1, stride_axis=0)
            tail = jnp.where(kept, corner, scores[:, breadth:])
            full = jnp.concatenate([scores[:, :breadth], tail], axis=1) * scale
            high, low = split(full)
            out_ref[b, 0, :, :DISP] = full
            out_ref[b, 0, :, DISP:] = dot(high, pool) + dot(low, pool)

    block = pl.BlockSpec((batch, 1, breadth, channels), lambda j: (0, j, 0, 0))
    operands = [left, own, near, far]
    specs = [block] * 3 + [pl.BlockSpec((batch // 2, 1, breadth, breadth), lambda j: (0, j, 0, 0))]
    aliases = {}
    if held is not None:
        operands.append(held)
        specs.append(pl.BlockSpec(memory_space=pl.ANY))
        aliases = {4: 0}
    return pl.pallas_call(
        kernel,
        grid=(count,),
        out_shape=jax.ShapeDtypeStruct((batch, height, breadth, width), F32),
        in_specs=specs,
        out_specs=pl.BlockSpec(
            (batch, 1, breadth, width), lambda j: (0, (j + first) % height, 0, 0)
        ),
        input_output_aliases=aliases,
        cost_estimate=cost(
            2 * batch * count * breadth * DISP * (channels + 2 * pooled),
            batch * count * breadth * (6 * channels + 4 * width),
        ),
        name="volume",
    )(*operands)


def shards(left_features, right_features, conv_weight, conv_bias):
    batch, height, breadth, channels = left_features.shape
    assert DISP == 2 * breadth and batch % 2 == 0
    both = (right_features, left_features)
    side = (
        shifted(jnp.stack([f[:, :, -1] for f in both]), "cols", 1),
        shifted(jnp.stack([f[:, :, 0] for f in both]), "cols", -1),
    )

    def edge(row):
        parts = [jnp.stack([f[:, row] for f in both])]
        parts += [s[:, :, row][:, :, None] for s in side]
        return jnp.concatenate(parts, axis=2)

    edges = (shifted(edge(-1), "rows", 1), shifted(edge(0), "rows", -1))
    half = height // 2
    groups = [list(range(1, 1 + half)), list(range(1 + half, height)) + [0]]
    weight, bias = conv_weight, conv_bias
    rights, lefts, nears, fars = [], [], [], []
    for rows in groups:
        outer = None if min(rows) > 0 and max(rows) < height - 1 else edges
        right = encode(right_features, side, outer, weight, bias, rows, 0, True)
        nears.append(shifted(right, "cols", 1))
        left = encode(left_features, side, outer, weight, bias, rows, 1, False)
        fars.append(shifted(left, "cols", -1))
        rights.append(right)
        lefts.append(left)
    corners = [shifted(triangle(l, r), "cols", 1) for l, r in zip(fars, nears)]
    out = None
    for k, rows in enumerate(groups):
        out = volume(lefts[k], rights[k], nears[k], corners[k], rows[0], height, out)
    return out


def solution(mesh):
    return jax.shard_map(
        shards,
        mesh=mesh,
        in_specs=(P(None, "rows", "cols", None), P(None, "rows", "cols", None), P(), P()),
        out_specs=P(None, "rows", "cols", None),
        check_vma=False,
    )
```

time: 129 us -> 93.6 us (0.73)
  Pallas kernels: 0 us -> 44.4 us
  waiting for transfers between devices: 40.8 us -> 3.01 us
  other arithmetic: 20.7 us -> 0.07 us
  matrix products: 14.9 us -> 0 us
  local copies, waits for them, and re-layouts: 23 us -> 16 us
    pallas_call x0 -> x8, Pallas kernels: none -> 44.4 us  [the longest x4 23.3 us: encode(): pl.pallas_call(kernel, out_shape=jax.ShapeDtypeStruct((batch, count, brea...]
    ppermute x10, waiting for transfers between devices: 40.8 us -> 3.01 us  [shifted(): lax.ppermute(value, axis, [(i, i + steps) for i in range(first, last)])]
    concatenate x5 -> x2, other arithmetic: 16.5 us -> 0.05 us  [edge(): return jnp.concatenate(parts, axis=2)]
    dot_general x19 -> x0, matrix products: 14.9 us -> none  [the longest x18 11.7 us: encode(): jnp.dot(window, conv_weight[row_tap, col_tap], preferred_element_type=jnp...]
    reshape x1 -> x0, local copies, waits for them, and re-layouts: 6.63 us -> none  [pyramid(): skewed = scores[..., 1:].reshape(leading + (-1,))]
    pallas_call x0 -> x1, local copies, waits for them, and re-layouts: none -> 6.42 us  [volume(): pl.pallas_call(kernel, grid=(count,), out_shape=jax.ShapeDtypeStruct((bat...]
    concatenate x3 -> x0, local copies, waits for them, and re-layouts: 3.66 us -> none  [the longest x1 3.64 us: pyramid(): return jnp.concatenate(levels, axis=-1)]
    pad x1 -> x0, local copies, waits for them, and re-layouts: 2.64 us -> none  [pyramid(): skewed = jnp.pad(skewed, [(0, 0)] * len(leading) + [(0, queries)])]
  transfers between devices with their start and end apart: 10 -> 10, of which waited for: 3 -> 2; matrix products, arithmetic and copies ran while one was open for 21% -> 2% of each run, Pallas kernels for 0% -> 40%
where the time goes in v1:
time: 93.6 us; the launch traced here: 92.7 us
  Pallas kernels  44.4 us (47%)
  starting transfers between devices  28.9 us (31%)
  local copies, waits for them, and re-layouts  16 us (17%)
  waiting for transfers between devices  3.01 us (3%)
    ppermute x10, starting transfers between devices, shifted(): lax.ppermute(value, axis, [(i, i + steps) for i in range(first, last)])  28.9 us
    pallas_call x4, Pallas kernels, encode(): pl.pallas_call(kernel, out_shape=jax.ShapeDtypeStruct((batch, count, brea...  23.3 us
    pallas_call x2, Pallas kernels, volume(): pl.pallas_call(kernel, grid=(count,), out_shape=jax.ShapeDtypeStruct((bat...  14.7 us
    pallas_call x2, Pallas kernels, triangle(): pl.pallas_call(kernel, out_shape=jax.ShapeDtypeStruct((batch // 2, count,...  6.48 us
    pallas_call x1, local copies, waits for them, and re-layouts, volume(): pl.pallas_call(kernel, grid=(count,), out_shape=jax.ShapeDtypeStruct((bat...  6.42 us
    unnamed x20, local copies, waits for them, and re-layouts  5.6 us
    ppermute x10, waiting for transfers between devices, shifted(): lax.ppermute(value, axis, [(i, i + steps) for i in range(first, last)])  3.01 us
    another operation x2, local copies, waits for them, and re-layouts, edge(): parts = [jnp.stack([f[:, row] for f in both])]  1.99 us
  transfers between devices with their start and end apart: 10, of which 2 were waited for; matrix products, arithmetic and copies ran while one was open for 2% of the time, Pallas kernels for 40%

profile of v1, /device:TPU:25, one launch (start us, length us, event | category | flops | bytes accessed | tf_op | source)
XLA Modules:
  0.0 92.7 jit_solution(6687982041539019766)
XLA Ops:
  1.0 1.0 %fusion = (bf16[2,12,1,256]{3,2,1,0:T(2,128)(2,1)S(1)}, bf16[2,12,1,256]{3,2,1,0:T(2,128)(2,1)S(1)}) fusion(bf16[2,12,128,256]{3,2,1,0:T(8,128)(2,1)} %image_ref.7), kind=kLoop, calls=%fused_computation.12 | loop fusion | bytes 49152 | tf_op jit(solution)/shard_map/slice | solution.py:197
  2.0 3.7 %collective-permute-start = (bf16[2,2,12,256]{3,2,1,0:T(8,128)(2,1)S(1)}, bf16[2,2,12,256]{3,2,1,0:T(8,128)(2,1)S(1)}, u32[]{:S(2)}, u32[]{:S(2)}) collective-permute-start(bf16[2,2,12,256]{3,2,1,0:T(8,128)(2,1)S(1)} %pad_maximum_fusion.2), channel_id=1, source_target_pairs={{0,1},{1,2},{2,3},{4,5},{5,6},{6,7},{8,9},{9,10},{10,11},{12,13},{... | collective-permute-start | bytes 73736 | tf_op jit(solution)/shard_map/ppermute | solution.py:20
  5.8 1.9 %collective-permute-start.1 = (bf16[2,2,12,256]{3,2,1,0:T(8,128)(2,1)S(1)}, bf16[2,2,12,256]{3,2,1,0:T(8,128)(2,1)S(1)}, u32[]{:S(2)}, u32[]{:S(2)}) collective-permute-start(bf16[2,2,12,256]{3,2,1,0:T(8,128)(2,1)S(1)} %pad_maximum_fusion.3), channel_id=1, source_target_pairs={{1,0},{2,1},{3,2},{5,4},{6,5},{7,6},{9,8},{10,9},{11,10},{13,12},{... | collective-permute-start | bytes 73736 | tf_op jit(solution)/shard_map/ppermute | solution.py:20
  7.7 1.0 %slice_bitcast_fusion = (bf16[1,2,128,256]{3,2,1,0:T(8,128)(2,1)S(1)}, bf16[1,2,128,256]{3,2,1,0:T(8,128)(2,1)S(1)}) fusion(bf16[2,12,128,256]{3,2,1,0:T(8,128)(2,1)} %image_ref.6), kind=kLoop, calls=%fused_computation.2 | loop fusion | bytes 524288 | tf_op jit(solution)/shard_map/stack;squeeze | solution.py:201
  8.7 1.0 %slice_bitcast_fusion.1 = (bf16[1,2,128,256]{3,2,1,0:T(8,128)(2,1)S(1)}, bf16[1,2,128,256]{3,2,1,0:T(8,128)(2,1)S(1)}) fusion(bf16[2,12,128,256]{3,2,1,0:T(8,128)(2,1)} %image_ref.7), kind=kLoop, calls=%fused_computation.3 | loop fusion | bytes 524288 | tf_op jit(solution)/shard_map/stack;squeeze | solution.py:201
  9.7 1.3 %collective-permute-done.1.after_ref = bf16[2,2,12,256]{3,2,1,0:T(8,128)(2,1)S(1)} collective-permute-done((bf16[2,2,12,256]{3,2,1,0:T(8,128)(2,1)S(1)}, bf16[2,2,12,256]{3,2,1,0:T(8,128)(2,1)S(1)}, u32[]{:S(2)}, u32[]{:S(2)}) %collective-permute-start.1) | collective-permute-done | bytes 24608 | tf_op jit(solution)/shard_map/ppermute | solution.py:20
  11.0 3.1 %collective-permute-start.2 = (bf16[2,2,130,256]{3,2,1,0:T(8,128)(2,1)S(1)}, bf16[2,2,130,256]{3,2,1,0:T(8,128)(2,1)S(1)}, u32[]{:S(2)}, u32[]{:S(2)}) collective-permute-start(bf16[2,2,130,256]{3,2,1,0:T(8,128)(2,1)S(1)} %pad_maximum_fusion), channel_id=1, source_target_pairs={{0,4},{4,8},{8,12},{12,16},{16,20},{20,24},{24,28},{1,5},{5,9},{9,... | collective-permute-start | bytes 798728 | tf_op jit(solution)/shard_map/ppermute | solution.py:20
  14.2 3.1 %collective-permute-start.3 = (bf16[2,2,130,256]{3,2,1,0:T(8,128)(2,1)S(1)}, bf16[2,2,130,256]{3,2,1,0:T(8,128)(2,1)S(1)}, u32[]{:S(2)}, u32[]{:S(2)}) collective-permute-start(bf16[2,2,130,256]{3,2,1,0:T(8,128)(2,1)S(1)} %pad_maximum_fusion.1), channel_id=1, source_target_pairs={{4,0},{8,4},{12,8},{16,12},{20,16},{24,20},{28,24},{5,1},{9,5},{13... | collective-permute-start | bytes 798728 | tf_op jit(solution)/shard_map/ppermute | solution.py:20
  17.3 6.8 %encode.7.refs_1_ = bf16[2,6,128,256]{3,2,1,0:T(8,128)(2,1)} custom-call(bf16[2,12,128,256]{3,2,1,0:T(8,128)(2,1)} %image_ref.7, bf16[2,2,12,256]{3,2,1,0:T(8,128)(2,1)} %copy-done.6, bf16[2,2,12,256]{3,2,1,0:T(8,128)(2,1)} %copy-done.7, bf16[3,768,256]{2,1,0:T(8,128)(2,1)} %bitcast.26, f32[1,256]{1,0:T(1,128)} %bitcast.30), custom_call_target="tpu_custom_call" | custom-call | flops 1811939328 | bytes 1572864 | tf_op jit(solution)/shard_map/encode/pallas_call | solution.py:91
  24.1 2.9 %collective-permute-start.7 = (bf16[2,6,128,256]{3,2,1,0:T(8,128)(2,1)}, bf16[2,6,128,256]{3,2,1,0:T(8,128)(2,1)S(1)}, u32[]{:S(2)}, u32[]{:S(2)}) collective-permute-start(bf16[2,6,128,256]{3,2,1,0:T(8,128)(2,1)} %encode.7.refs_1_), channel_id=1, source_target_pairs={{0,1},{1,2},{2,3},{4,5},{5,6},{6,7},{8,9},{9,10},{10,11},{12,13},{... | collective-permute-start | bytes 2359304 | tf_op jit(solution)/shard_map/ppermute | solution.py:20
  27.1 4.7 %encode.6.refs_0_ = bf16[2,6,128,256]{3,2,1,0:T(8,128)(2,1)} custom-call(bf16[2,12,128,256]{3,2,1,0:T(8,128)(2,1)} %image_ref.6, bf16[2,2,12,256]{3,2,1,0:T(8,128)(2,1)} %copy-done.6, bf16[2,2,12,256]{3,2,1,0:T(8,128)(2,1)} %copy-done.7, bf16[3,768,256]{2,1,0:T(8,128)(2,1)} %bitcast.27, f32[1,256]{1,0:T(1,128)} %bitcast.31), custom_call_target="tpu_custom_call" | custom-call | flops 1811939328 | bytes 1572864 | tf_op jit(solution)/shard_map/encode/pallas_call | solution.py:91
  31.8 1.9 %collective-permute-start.8 = (bf16[2,6,128,256]{3,2,1,0:T(8,128)(2,1)}, bf16[2,6,128,256]{3,2,1,0:T(8,128)(2,1)S(1)}, u32[]{:S(2)}, u32[]{:S(2)}) collective-permute-start(bf16[2,6,128,256]{3,2,1,0:T(8,128)(2,1)} %encode.6.refs_0_), channel_id=1, source_target_pairs={{1,0},{2,1},{3,2},{5,4},{6,5},{7,6},{9,8},{10,9},{11,10},{13,12},{... | collective-permute-start | bytes 2359304 | tf_op jit(solution)/shard_map/ppermute | solution.py:20
  35.2 4.8 %encode.4.refs_0_ = bf16[2,6,128,256]{3,2,1,0:T(8,128)(2,1)} custom-call(bf16[2,12,128,256]{3,2,1,0:T(8,128)(2,1)} %image_ref.6, bf16[2,2,12,256]{3,2,1,0:T(8,128)(2,1)} %copy-done.6, bf16[2,2,12,256]{3,2,1,0:T(8,128)(2,1)} %copy-done.7, bf16[2,2,130,256]{3,2,1,0:T(8,128)(2,1)} %copy-done.8, bf16[2,2,130,256]{3,2,1,0:T(8,128)(2,1)} %copy-done.9, ...), custom_call_target="tpu_custom_call" | custom-call | flops 1811939328 | bytes 1572864 | tf_op jit(solution)/shard_map/encode/pallas_call | solution.py:91
  40.0 1.9 %collective-permute-start.5 = (bf16[2,6,128,256]{3,2,1,0:T(8,128)(2,1)}, bf16[2,6,128,256]{3,2,1,0:T(8,128)(2,1)S(1)}, u32[]{:S(2)}, u32[]{:S(2)}) collective-permute-start(bf16[2,6,128,256]{3,2,1,0:T(8,128)(2,1)} %encode.4.refs_0_), channel_id=1, source_target_pairs={{1,0},{2,1},{3,2},{5,4},{6,5},{7,6},{9,8},{10,9},{11,10},{13,12},{... | collective-permute-start | bytes 2359304 | tf_op jit(solution)/shard_map/ppermute | solution.py:20
  41.9 6.9 %encode.5.refs_1_ = bf16[2,6,128,256]{3,2,1,0:T(8,128)(2,1)} custom-call(bf16[2,12,128,256]{3,2,1,0:T(8,128)(2,1)} %image_ref.7, bf16[2,2,12,256]{3,2,1,0:T(8,128)(2,1)} %copy-done.6, bf16[2,2,12,256]{3,2,1,0:T(8,128)(2,1)} %copy-done.7, bf16[2,2,130,256]{3,2,1,0:T(8,128)(2,1)} %copy-done.8, bf16[2,2,130,256]{3,2,1,0:T(8,128)(2,1)} %copy-done.9, ...), custom_call_target="tpu_custom_call" | custom-call | flops 1811939328 | bytes 1572864 | tf_op jit(solution)/shard_map/encode/pallas_call | solution.py:91
  48.8 3.6 %collective-permute-start.4 = (bf16[2,6,128,256]{3,2,1,0:T(8,128)(2,1)}, bf16[2,6,128,256]{3,2,1,0:T(8,128)(2,1)S(1)}, u32[]{:S(2)}, u32[]{:S(2)}) collective-permute-start(bf16[2,6,128,256]{3,2,1,0:T(8,128)(2,1)} %encode.5.refs_1_), channel_id=1, source_target_pairs={{0,1},{1,2},{2,3},{4,5},{5,6},{6,7},{8,9},{9,10},{10,11},{12,13},{... | collective-permute-start | bytes 2359304 | tf_op jit(solution)/shard_map/ppermute | solution.py:20
  54.3 3.2 %triangle.3 = f32[1,6,128,128]{3,2,1,0:T(8,128)} custom-call(bf16[2,6,128,256]{3,2,1,0:T(8,128)(2,1)} %copy-done.2, bf16[2,6,128,256]{3,2,1,0:T(8,128)(2,1)} %copy-done), custom_call_target="tpu_custom_call" | custom-call | flops 100663296 | bytes 1572864 | tf_op jit(solution)/shard_map/triangle/pallas_call | solution.py:116
  57.5 2.4 %collective-permute-start.9 = (f32[1,6,128,128]{3,2,1,0:T(8,128)}, f32[1,6,128,128]{3,2,1,0:T(8,128)S(1)}, u32[]{:S(2)}, u32[]{:S(2)}) collective-permute-start(f32[1,6,128,128]{3,2,1,0:T(8,128)} %triangle.3), channel_id=1, source_target_pairs={{0,1},{1,2},{2,3},{4,5},{5,6},{6,7},{8,9},{9,10},{10,11},{12,13},{... | collective-permute-start | bytes 1179656 | tf_op jit(solution)/shard_map/ppermute | solution.py:20
  60.0 1.7 %collective-permute-done.4.right_ref.refs_2_ = bf16[2,6,128,256]{3,2,1,0:T(8,128)(2,1)S(1)} collective-permute-done((bf16[2,6,128,256]{3,2,1,0:T(8,128)(2,1)}, bf16[2,6,128,256]{3,2,1,0:T(8,128)(2,1)S(1)}, u32[]{:S(2)}, u32[]{:S(2)}) %collective-permute-start.4) | collective-permute-done | bytes 786464 | tf_op jit(solution)/shard_map/ppermute | solution.py:20
  62.6 3.2 %triangle.2 = f32[1,6,128,128]{3,2,1,0:T(8,128)} custom-call(bf16[2,6,128,256]{3,2,1,0:T(8,128)(2,1)} %copy-done.3, bf16[2,6,128,256]{3,2,1,0:T(8,128)(2,1)} %copy-done.1), custom_call_target="tpu_custom_call" | custom-call | flops 100663296 | bytes 1572864 | tf_op jit(solution)/shard_map/triangle/pallas_call | solution.py:116
  65.9 4.3 %collective-permute-start.6 = (f32[1,6,128,128]{3,2,1,0:T(8,128)}, f32[1,6,128,128]{3,2,1,0:T(8,128)S(1)}, u32[]{:S(2)}, u32[]{:S(2)}) collective-permute-start(f32[1,6,128,128]{3,2,1,0:T(8,128)} %triangle.2), channel_id=1, source_target_pairs={{0,1},{1,2},{2,3},{4,5},{5,6},{6,7},{8,9},{9,10},{10,11},{12,13},{... | collective-permute-start | bytes 1179656 | tf_op jit(solution)/shard_map/ppermute | solution.py:20
  70.9 7.3 %volume.2.refs_4_ = f32[2,12,128,480]{3,2,1,0:T(8,128)} custom-call(bf16[2,6,128,256]{3,2,1,0:T(8,128)(2,1)} %encode.6.refs_0_, bf16[2,6,128,256]{3,2,1,0:T(8,128)(2,1)} %encode.7.refs_1_, bf16[2,6,128,256]{3,2,1,0:T(8,128)(2,1)} %copy-done, f32[1,6,128,128]{3,2,1,0:T(8,128)} %copy-done.4), custom_call_target="tpu_custom_call" | custom-call | flops 553648128 | bytes 5308416 | tf_op jit(solution)/shard_map/volume/pallas_call | solution.py:174
  79.0 7.3 %volume.3 = f32[2,12,128,480]{3,2,1,0:T(8,128)} custom-call(bf16[2,6,128,256]{3,2,1,0:T(8,128)(2,1)} %encode.4.refs_0_, bf16[2,6,128,256]{3,2,1,0:T(8,128)(2,1)} %encode.5.refs_1_, bf16[2,6,128,256]{3,2,1,0:T(8,128)(2,1)} %copy-done.1, f32[1,6,128,128]{3,2,1,0:T(8,128)} %copy-done.5, f32[2,12,128,480]{3,2,1,0:T(8,128)} %volume.2.refs_4_), custom_call_target="tpu_custom_call", output_to_operand_aliasing={{}: (4, {})} | custom-call | flops 553648128 | bytes 5308416 | tf_op jit(solution)/shard_map/volume/pallas_call | solution.py:174
  86.3 6.4 %copy.14 = f32[2,12,128,480]{2,3,1,0:T(8,128)} copy(f32[2,12,128,480]{3,2,1,0:T(8,128)} %volume.3) | data formatting | bytes 11796480 | tf_op jit(solution)/shard_map/volume/pallas_call | solution.py:174
  (37 shorter events, 6.7 us)
Async XLA Ops:
  2.0 7.7 %collective-permute-start = (bf16[2,2,12,256]{3,2,1,0:T(8,128)(2,1)S(1)}, bf16[2,2,12,256]{3,2,1,0:T(8,128)(2,1)S(1)}, u32[]{:S(2)}, u32[]{:S(2)}) collective-permute-start(bf16[2,2,12,256]{3,2,1,0:T(8,128)(2,1)S(1)} %pad_maximum_fusion.2), channel_id=1, source_target_pairs={{0,1},{1,2},{2,3},{4,5},{5,6},{6,7},{8,9},{9,10},{10,11},{12,13},{... | collective-permute-start | bytes 73736 | tf_op jit(solution)/shard_map/ppermute | solution.py:20
  5.8 5.2 %collective-permute-start.1 = (bf16[2,2,12,256]{3,2,1,0:T(8,128)(2,1)S(1)}, bf16[2,2,12,256]{3,2,1,0:T(8,128)(2,1)S(1)}, u32[]{:S(2)}, u32[]{:S(2)}) collective-permute-start(bf16[2,2,12,256]{3,2,1,0:T(8,128)(2,1)S(1)} %pad_maximum_fusion.3), channel_id=1, source_target_pairs={{1,0},{2,1},{3,2},{5,4},{6,5},{7,6},{9,8},{10,9},{11,10},{13,12},{... | collective-permute-start | bytes 73736 | tf_op jit(solution)/shard_map/ppermute | solution.py:20
  9.7 7.6 %copy-start.6 = (bf16[2,2,12,256]{3,2,1,0:T(8,128)(2,1)}, bf16[2,2,12,256]{3,2,1,0:T(8,128)(2,1)S(1)}, u32[]{:S(2)}) copy-start(bf16[2,2,12,256]{3,2,1,0:T(8,128)(2,1)S(1)} %collective-permute-done.before_ref) | copy-start | bytes 73732
  11.0 6.3 %copy-start.7 = (bf16[2,2,12,256]{3,2,1,0:T(8,128)(2,1)}, bf16[2,2,12,256]{3,2,1,0:T(8,128)(2,1)S(1)}, u32[]{:S(2)}) copy-start(bf16[2,2,12,256]{3,2,1,0:T(8,128)(2,1)S(1)} %collective-permute-done.1.after_ref) | copy-start | bytes 73732
  11.0 22.7 %collective-permute-start.2 = (bf16[2,2,130,256]{3,2,1,0:T(8,128)(2,1)S(1)}, bf16[2,2,130,256]{3,2,1,0:T(8,128)(2,1)S(1)}, u32[]{:S(2)}, u32[]{:S(2)}) collective-permute-start(bf16[2,2,130,256]{3,2,1,0:T(8,128)(2,1)S(1)} %pad_maximum_fusion), channel_id=1, source_target_pairs={{0,4},{4,8},{8,12},{12,16},{16,20},{20,24},{24,28},{1,5},{5,9},{9,... | collective-permute-start | bytes 798728 | tf_op jit(solution)/shard_map/ppermute | solution.py:20
  14.2 19.5 %collective-permute-start.3 = (bf16[2,2,130,256]{3,2,1,0:T(8,128)(2,1)S(1)}, bf16[2,2,130,256]{3,2,1,0:T(8,128)(2,1)S(1)}, u32[]{:S(2)}, u32[]{:S(2)}) collective-permute-start(bf16[2,2,130,256]{3,2,1,0:T(8,128)(2,1)S(1)} %pad_maximum_fusion.1), channel_id=1, source_target_pairs={{4,0},{8,4},{12,8},{16,12},{20,16},{24,20},{28,24},{5,1},{9,5},{13... | collective-permute-start | bytes 798728 | tf_op jit(solution)/shard_map/ppermute | solution.py:20
  24.1 28.3 %collective-permute-start.7 = (bf16[2,6,128,256]{3,2,1,0:T(8,128)(2,1)}, bf16[2,6,128,256]{3,2,1,0:T(8,128)(2,1)S(1)}, u32[]{:S(2)}, u32[]{:S(2)}) collective-permute-start(bf16[2,6,128,256]{3,2,1,0:T(8,128)(2,1)} %encode.7.refs_1_), channel_id=1, source_target_pairs={{0,1},{1,2},{2,3},{4,5},{5,6},{6,7},{8,9},{9,10},{10,11},{12,13},{... | collective-permute-start | bytes 2359304 | tf_op jit(solution)/shard_map/ppermute | solution.py:20
  31.8 20.7 %collective-permute-start.8 = (bf16[2,6,128,256]{3,2,1,0:T(8,128)(2,1)}, bf16[2,6,128,256]{3,2,1,0:T(8,128)(2,1)S(1)}, u32[]{:S(2)}, u32[]{:S(2)}) collective-permute-start(bf16[2,6,128,256]{3,2,1,0:T(8,128)(2,1)} %encode.6.refs_0_), channel_id=1, source_target_pairs={{1,0},{2,1},{3,2},{5,4},{6,5},{7,6},{9,8},{10,9},{11,10},{13,12},{... | collective-permute-start | bytes 2359304 | tf_op jit(solution)/shard_map/ppermute | solution.py:20
  33.7 0.7 copy-start.8
  34.4 0.7 copy-start.9
  40.0 20.0 %collective-permute-start.5 = (bf16[2,6,128,256]{3,2,1,0:T(8,128)(2,1)}, bf16[2,6,128,256]{3,2,1,0:T(8,128)(2,1)S(1)}, u32[]{:S(2)}, u32[]{:S(2)}) collective-permute-start(bf16[2,6,128,256]{3,2,1,0:T(8,128)(2,1)} %encode.4.refs_0_), channel_id=1, source_target_pairs={{1,0},{2,1},{3,2},{5,4},{6,5},{7,6},{9,8},{10,9},{11,10},{13,12},{... | collective-permute-start | bytes 2359304 | tf_op jit(solution)/shard_map/ppermute | solution.py:20
  48.8 12.9 %collective-permute-start.4 = (bf16[2,6,128,256]{3,2,1,0:T(8,128)(2,1)}, bf16[2,6,128,256]{3,2,1,0:T(8,128)(2,1)S(1)}, u32[]{:S(2)}, u32[]{:S(2)}) collective-permute-start(bf16[2,6,128,256]{3,2,1,0:T(8,128)(2,1)} %encode.5.refs_1_), channel_id=1, source_target_pairs={{0,1},{1,2},{2,3},{4,5},{5,6},{6,7},{8,9},{9,10},{10,11},{12,13},{... | collective-permute-start | bytes 2359304 | tf_op jit(solution)/shard_map/ppermute | solution.py:20
  52.5 0.9 copy-start
  53.3 0.9 copy-start.2
  57.5 12.6 %collective-permute-start.9 = (f32[1,6,128,128]{3,2,1,0:T(8,128)}, f32[1,6,128,128]{3,2,1,0:T(8,128)S(1)}, u32[]{:S(2)}, u32[]{:S(2)}) collective-permute-start(f32[1,6,128,128]{3,2,1,0:T(8,128)} %triangle.3), channel_id=1, source_target_pairs={{0,1},{1,2},{2,3},{4,5},{5,6},{6,7},{8,9},{9,10},{10,11},{12,13},{... | collective-permute-start | bytes 1179656 | tf_op jit(solution)/shard_map/ppermute | solution.py:20
  60.0 1.7 %copy-start.3 = (bf16[2,6,128,256]{3,2,1,0:T(8,128)(2,1)}, bf16[2,6,128,256]{3,2,1,0:T(8,128)(2,1)S(1)}, u32[]{:S(2)}) copy-start(bf16[2,6,128,256]{3,2,1,0:T(8,128)(2,1)S(1)} %collective-permute-done.5.left_ref) | copy-start | bytes 2359300
  61.7 0.9 copy-start.1
  65.9 12.4 %collective-permute-start.6 = (f32[1,6,128,128]{3,2,1,0:T(8,128)}, f32[1,6,128,128]{3,2,1,0:T(8,128)S(1)}, u32[]{:S(2)}, u32[]{:S(2)}) collective-permute-start(f32[1,6,128,128]{3,2,1,0:T(8,128)} %triangle.2), channel_id=1, source_target_pairs={{0,1},{1,2},{2,3},{4,5},{5,6},{6,7},{8,9},{9,10},{10,11},{12,13},{... | collective-permute-start | bytes 1179656 | tf_op jit(solution)/shard_map/ppermute | solution.py:20
  70.1 0.8 copy-start.4
  78.2 0.7 copy-start.5

commit v2 on v1

v2 whole, which is shorter than its diff:
```python
import math

import jax
import jax.numpy as jnp
import numpy as np
from jax import lax
from jax.experimental import pallas as pl
from jax.experimental.pallas import tpu as pltpu
from jax.sharding import PartitionSpec as P

DISP = 256
LEVELS = 4
F32 = jnp.float32
BF16 = jnp.bfloat16


def shifted(value, axis, steps):
    count = lax.axis_size(axis)
    first, last = max(0, -steps), min(count, count - steps)
    return lax.ppermute(value, axis, [(i, i + steps) for i in range(first, last)])


def iota(shape, dim):
    return lax.broadcasted_iota(jnp.int32, shape, dim)


def reversal(size):
    mirrored = iota((size, size), 0) + iota((size, size), 1) == size - 1
    return jnp.where(mirrored, 1.0, 0.0).astype(BF16)


def dot(a, b):
    return jnp.dot(a, b, preferred_element_type=F32)


def dot_t(a, b):
    return lax.dot_general(a, b, (((1,), (1,)), ((), ())), preferred_element_type=F32)


def in_hbm(value):
    return pltpu.with_memory_space_constraint(value, pltpu.HBM)


def cost(flops, nbytes):
    return pl.CostEstimate(flops=flops, bytes_accessed=nbytes, transcendentals=0)


def encode(image, side, edges, weight, bias, rows, which, mirror):
    batch, height, breadth, channels = image.shape
    count = len(rows)
    needed = sorted({r + dy for r in rows for dy in (-1, 0, 1)})
    place = {r: i for i, r in enumerate(needed)}

    def kernel(image_ref, before_ref, after_ref, *rest):
        if edges is None:
            weight_ref, bias_ref, out_ref, taps = rest
        else:
            up_ref, down_ref, weight_ref, bias_ref, out_ref, taps = rest
        spot = iota((breadth, channels), 0)
        for r in needed:
            if 0 <= r < height:
                row = image_ref[0, r]
                before = before_ref[0, 0, r : r + 1, :]
                after = after_ref[0, 0, r : r + 1, :]
            else:
                ref = up_ref if r < 0 else down_ref
                row = ref[0, 0, :breadth, :]
                ends = ref[0, 0, breadth:, :]
                before = ends[0:1]
                after = ends[1:2]
            wide = row.astype(F32)
            west = jnp.where(spot == 0, before.astype(F32), pltpu.roll(wide, 1, 0))
            east = jnp.where(
                spot == breadth - 1, after.astype(F32), pltpu.roll(wide, breadth - 1, 0)
            )
            taps[place[r], :, :channels] = west.astype(BF16)
            taps[place[r], :, channels : 2 * channels] = row
            taps[place[r], :, 2 * channels :] = east.astype(BF16)
        total = None
        for dy in range(3):
            window = jnp.concatenate([taps[place[r + dy - 1]] for r in rows], axis=0)
            part = dot(window, weight_ref[dy])
            total = part if total is None else total + part
        centre = jnp.concatenate([image_ref[0, r] for r in rows], axis=0).astype(F32)
        encoded = (centre + jnp.maximum(total + bias_ref[...], 0.0)).astype(BF16)
        values = [encoded[i * breadth : (i + 1) * breadth] for i in range(count)]
        if mirror:
            flip = reversal(breadth)
            values = [dot(flip, value).astype(BF16) for value in values]
        for i in range(count):
            out_ref[0, i] = values[i]

    operands = [image, side[0], side[1]] + ([] if edges is None else list(edges))
    operands += [weight.reshape(3, 3 * channels, channels), bias.reshape(1, channels)]
    picked = [pl.BlockSpec((1, 1) + a.shape[2:], lambda b: (which, b, 0, 0)) for a in operands[1:-2]]
    return pl.pallas_call(
        kernel,
        grid=(batch,),
        out_shape=jax.ShapeDtypeStruct((batch, count, breadth, channels), BF16),
        in_specs=[pl.BlockSpec((1, height, breadth, channels), lambda b: (b, 0, 0, 0))]
        + picked
        + [
            pl.BlockSpec((3, 3 * channels, channels), lambda b: (0, 0, 0)),
            pl.BlockSpec((1, channels), lambda b: (0, 0)),
        ],
        out_specs=pl.BlockSpec((1, count, breadth, channels), lambda b: (b, 0, 0, 0)),
        scratch_shapes=[pltpu.VMEM((len(needed), breadth, 3 * channels), BF16)],
        cost_estimate=cost(batch * count * breadth * channels * channels * 18, 2 * image.size),
        name="encode",
    )(*operands)


def triangle(left, right):
    batch, count, breadth, channels = left.shape

    def kernel(left_ref, right_ref, out_ref):
        near = iota((breadth, breadth), 1) > iota((breadth, breadth), 0)
        flip = reversal(breadth)
        for i in range(2):
            for b in range(0, batch, 2):
                upper = dot_t(left_ref[b, i], right_ref[b, i])
                upper = pltpu.roll(upper, 1, 1, stride=1, stride_axis=0)
                turned = dot(flip, left_ref[b + 1, i]).astype(BF16)
                lower = dot_t(turned, right_ref[b + 1, i])
                out_ref[b // 2, i] = jnp.where(near, upper, lower)

    return pl.pallas_call(
        kernel,
        grid=(count // 2,),
        out_shape=jax.ShapeDtypeStruct((batch // 2, count, breadth, breadth), F32),
        in_specs=[pl.BlockSpec((batch, 2, breadth, channels), lambda j: (0, j, 0, 0))] * 2,
        out_specs=pl.BlockSpec((batch // 2, 2, breadth, breadth), lambda j: (0, j, 0, 0)),
        cost_estimate=cost(2 * batch * count * breadth * breadth * channels, 4 * left.size),
        name="triangle",
    )(in_hbm(left), in_hbm(right))


def split(value):
    high = value.astype(BF16)
    return high, (value - high.astype(F32)).astype(BF16)


def pooling():
    rows = [np.zeros((0, DISP), np.float32)]
    for level in range(1, LEVELS):
        size = DISP >> level
        groups = np.arange(DISP)[None, :] >> level == np.arange(size)[:, None]
        rows.append(groups.astype(np.float32) / (1 << level))
    return np.concatenate(rows, axis=0)


def volume(left, own, near, far, first, height, held):
    batch, count, breadth, channels = left.shape
    pool = jnp.asarray(pooling(), BF16)
    pooled = pool.shape[0]
    width = DISP + pooled
    scale = 1.0 / math.sqrt(channels)

    def kernel(*refs):
        left_ref, own_ref, near_ref, far_ref, pool_ref = refs[:5]
        out_ref = refs[-1]
        kept = iota((breadth, breadth), 1) > iota((breadth, breadth), 0)
        flip = reversal(breadth)
        spots = [(b, i) for i in range(2) for b in range(batch)]
        scores, corners, fulls = {}, {}, {}
        for b, i in spots:
            window = jnp.concatenate([own_ref[b, i], near_ref[b, i]], axis=0)
            scores[b, i] = dot_t(left_ref[b, i], window)
        for b, i in spots:
            corners[b, i] = far_ref[b // 2, i]
            if b % 2:
                high, low = split(corners[b, i])
                corners[b, i] = dot(flip, high) + dot(flip, low)
        for b, i in spots:
            turned = pltpu.roll(scores[b, i], breadth + 1, 1, stride=1, stride_axis=0)
            corner = corners[b, i]
            if b % 2:
                corner = pltpu.roll(corner, 1, 1, stride=1, stride_axis=0)
            tail = jnp.where(kept, corner, turned[:, breadth:])
            fulls[b, i] = jnp.concatenate([turned[:, :breadth], tail], axis=1) * scale
        for i in range(2):
            for b in range(0, batch, 2):
                high, low = split(jnp.concatenate([fulls[b, i], fulls[b + 1, i]], axis=0))
                means = dot_t(pool_ref[...], high) + dot_t(pool_ref[...], low)
                out_ref[b, i, DISP:, :] = means[:, :breadth]
                out_ref[b + 1, i, DISP:, :] = means[:, breadth:]
        for b, i in spots:
            out_ref[b, i, :DISP, :] = fulls[b, i].T

    block = pl.BlockSpec((batch, 2, breadth, channels), lambda j: (0, j, 0, 0))
    operands = [left, own, in_hbm(near), in_hbm(far), pool]
    specs = [block] * 3 + [pl.BlockSpec((batch // 2, 2, breadth, breadth), lambda j: (0, j, 0, 0))]
    specs.append(pl.BlockSpec((pooled, DISP), lambda j: (0, 0)))
    aliases = {}
    if held is not None:
        operands.append(held)
        specs.append(pl.BlockSpec(memory_space=pl.ANY))
        aliases = {5: 0}
    return pl.pallas_call(
        kernel,
        grid=(count // 2,),
        out_shape=jax.ShapeDtypeStruct((batch, height, width, breadth), F32),
        in_specs=specs,
        out_specs=pl.BlockSpec(
            (batch, 2, width, breadth), lambda j: (0, (j + first // 2) % (height // 2), 0, 0)
        ),
        input_output_aliases=aliases,
        cost_estimate=cost(
            2 * batch * count * breadth * DISP * (channels + 2 * pooled),
            batch * count * breadth * (6 * channels + 4 * width),
        ),
        name="volume",
    )(*operands)


def shards(left_features, right_features, conv_weight, conv_bias):
    batch, height, breadth, channels = left_features.shape
    assert DISP == 2 * breadth and batch % 2 == 0 and height % 4 == 0
    both = (right_features, left_features)
    side = (
        shifted(jnp.stack([f[:, :, -1] for f in both]), "cols", 1),
        shifted(jnp.stack([f[:, :, 0] for f in both]), "cols", -1),
    )

    def edge(row):
        parts = [jnp.stack([f[:, row] for f in both])]
        parts += [s[:, :, row][:, :, None] for s in side]
        return jnp.concatenate(parts, axis=2)

    edges = (shifted(edge(-1), "rows", 1), shifted(edge(0), "rows", -1))
    half = height // 2
    groups = [list(range(2, 2 + half)), list(range(2 + half, height)) + [0, 1]]
    weight, bias = conv_weight, conv_bias
    rights, lefts, nears, fars = [], [], [], []
    for rows in groups:
        outer = None if min(rows) > 0 and max(rows) < height - 1 else edges
        right = encode(right_features, side, outer, weight, bias, rows, 0, True)
        nears.append(shifted(right, "cols", 1))
        left = encode(left_features, side, outer, weight, bias, rows, 1, False)
        fars.append(shifted(left, "cols", -1))
        rights.append(right)
        lefts.append(left)
    corners = [shifted(triangle(l, r), "cols", 1) for l, r in zip(fars, nears)]
    out = None
    for k, rows in enumerate(groups):
        out = volume(lefts[k], rights[k], nears[k], corners[k], rows[0], height, out)
    return jnp.swapaxes(out, 2, 3)


def solution(mesh):
    return jax.shard_map(
        shards,
        mesh=mesh,
        in_specs=(P(None, "rows", "cols", None), P(None, "rows", "cols", None), P(), P()),
        out_specs=P(None, "rows", "cols", None),
        check_vma=False,
    )
```

time: 93.6 us -> 79.3 us (0.85)
  Pallas kernels: 44.4 us -> 37 us
  local copies, waits for them, and re-layouts: 16 us -> 9.6 us
    pallas_call x8, Pallas kernels: 44.4 us -> 37 us  [the longest x4 19.4 us: encode(): pl.pallas_call(kernel, grid=(batch,), out_shape=jax.ShapeDtypeStruct((bat...]
    pallas_call x1 -> x0, local copies, waits for them, and re-layouts: 6.42 us -> none  [volume(): pl.pallas_call(kernel, grid=(count,), out_shape=jax.ShapeDtypeStruct((bat...]
  transfers between devices with their start and end apart: 10 -> 10, of which waited for: 2 -> 2; matrix products, arithmetic and copies ran while one was open for 2% -> 3% of each run, Pallas kernels for 40% -> 41%
where the time goes in v2:
time: 79.3 us; the launch traced here: 78.5 us
  Pallas kernels  37 us (47%)
  starting transfers between devices  28.9 us (36%)
  local copies, waits for them, and re-layouts  9.6 us (12%)
  waiting for transfers between devices  2.62 us (3%)
    ppermute x10, starting transfers between devices, shifted(): lax.ppermute(value, axis, [(i, i + steps) for i in range(first, last)])  28.9 us
    pallas_call x4, Pallas kernels, encode(): pl.pallas_call(kernel, grid=(batch,), out_shape=jax.ShapeDtypeStruct((bat...  19.4 us
    pallas_call x2, Pallas kernels, volume(): pl.pallas_call(kernel, grid=(count // 2,), out_shape=jax.ShapeDtypeStruct...  10.3 us
    pallas_call x2, Pallas kernels, triangle(): pl.pallas_call(kernel, grid=(count // 2,), out_shape=jax.ShapeDtypeStruct...  7.33 us
    unnamed x20, local copies, waits for them, and re-layouts  5.61 us
    ppermute x10, waiting for transfers between devices, shifted(): lax.ppermute(value, axis, [(i, i + steps) for i in range(first, last)])  2.62 us
    another operation x2, local copies, waits for them, and re-layouts, edge(): parts = [jnp.stack([f[:, row] for f in both])]  1.99 us
    slice x2, local copies, waits for them, and re-layouts, shards(): f[:, :, 0]  1.97 us
  transfers between devices with their start and end apart: 10, of which 2 were waited for; matrix products, arithmetic and copies ran while one was open for 3% of the time, Pallas kernels for 41%

profile of v2, /device:TPU:25, one launch (start us, length us, event | category | flops | bytes accessed | tf_op | source)
XLA Modules:
  0.0 78.5 jit_solution(13802162790875891691)
XLA Ops:
  0.0 1.0 %fusion.1 = (bf16[2,12,1,256]{3,2,1,0:T(2,128)(2,1)S(1)}, bf16[2,12,1,256]{3,2,1,0:T(2,128)(2,1)S(1)}) fusion(bf16[2,12,128,256]{3,2,1,0:T(8,128)(2,1)} %image_ref.6), kind=kLoop, calls=%fused_computation.13 | loop fusion | bytes 49152 | tf_op jit(solution)/shard_map/slice | solution.py:222
  1.0 1.0 %fusion = (bf16[2,12,1,256]{3,2,1,0:T(2,128)(2,1)S(1)}, bf16[2,12,1,256]{3,2,1,0:T(2,128)(2,1)S(1)}) fusion(bf16[2,12,128,256]{3,2,1,0:T(8,128)(2,1)} %image_ref.7), kind=kLoop, calls=%fused_computation.12 | loop fusion | bytes 49152 | tf_op jit(solution)/shard_map/slice | solution.py:222
  2.0 3.7 %collective-permute-start = (bf16[2,2,12,256]{3,2,1,0:T(8,128)(2,1)S(1)}, bf16[2,2,12,256]{3,2,1,0:T(8,128)(2,1)S(1)}, u32[]{:S(2)}, u32[]{:S(2)}) collective-permute-start(bf16[2,2,12,256]{3,2,1,0:T(8,128)(2,1)S(1)} %pad_maximum_fusion.2), channel_id=1, source_target_pairs={{0,1},{1,2},{2,3},{4,5},{5,6},{6,7},{8,9},{9,10},{10,11},{12,13},{... | collective-permute-start | bytes 73736 | tf_op jit(solution)/shard_map/ppermute | solution.py:20
  5.8 1.9 %collective-permute-start.1 = (bf16[2,2,12,256]{3,2,1,0:T(8,128)(2,1)S(1)}, bf16[2,2,12,256]{3,2,1,0:T(8,128)(2,1)S(1)}, u32[]{:S(2)}, u32[]{:S(2)}) collective-permute-start(bf16[2,2,12,256]{3,2,1,0:T(8,128)(2,1)S(1)} %pad_maximum_fusion.3), channel_id=1, source_target_pairs={{1,0},{2,1},{3,2},{5,4},{6,5},{7,6},{9,8},{10,9},{11,10},{13,12},{... | collective-permute-start | bytes 73736 | tf_op jit(solution)/shard_map/ppermute | solution.py:20
  7.7 1.0 %slice_bitcast_fusion = (bf16[1,2,128,256]{3,2,1,0:T(8,128)(2,1)S(1)}, bf16[1,2,128,256]{3,2,1,0:T(8,128)(2,1)S(1)}) fusion(bf16[2,12,128,256]{3,2,1,0:T(8,128)(2,1)} %image_ref.6), kind=kLoop, calls=%fused_computation.2 | loop fusion | bytes 524288 | tf_op jit(solution)/shard_map/stack;squeeze | solution.py:226
  8.7 1.0 %slice_bitcast_fusion.1 = (bf16[1,2,128,256]{3,2,1,0:T(8,128)(2,1)S(1)}, bf16[1,2,128,256]{3,2,1,0:T(8,128)(2,1)S(1)}) fusion(bf16[2,12,128,256]{3,2,1,0:T(8,128)(2,1)} %image_ref.7), kind=kLoop, calls=%fused_computation.3 | loop fusion | bytes 524288 | tf_op jit(solution)/shard_map/stack;squeeze | solution.py:226
  9.7 1.3 %collective-permute-done.1.after_ref = bf16[2,2,12,256]{3,2,1,0:T(8,128)(2,1)S(1)} collective-permute-done((bf16[2,2,12,256]{3,2,1,0:T(8,128)(2,1)S(1)}, bf16[2,2,12,256]{3,2,1,0:T(8,128)(2,1)S(1)}, u32[]{:S(2)}, u32[]{:S(2)}) %collective-permute-start.1) | collective-permute-done | bytes 24608 | tf_op jit(solution)/shard_map/ppermute | solution.py:20
  11.0 3.1 %collective-permute-start.2 = (bf16[2,2,130,256]{3,2,1,0:T(8,128)(2,1)S(1)}, bf16[2,2,130,256]{3,2,1,0:T(8,128)(2,1)S(1)}, u32[]{:S(2)}, u32[]{:S(2)}) collective-permute-start(bf16[2,2,130,256]{3,2,1,0:T(8,128)(2,1)S(1)} %pad_maximum_fusion), channel_id=1, source_target_pairs={{0,4},{4,8},{8,12},{12,16},{16,20},{20,24},{24,28},{1,5},{5,9},{9,... | collective-permute-start | bytes 798728 | tf_op jit(solution)/shard_map/ppermute | solution.py:20
  14.2 3.1 %collective-permute-start.3 = (bf16[2,2,130,256]{3,2,1,0:T(8,128)(2,1)S(1)}, bf16[2,2,130,256]{3,2,1,0:T(8,128)(2,1)S(1)}, u32[]{:S(2)}, u32[]{:S(2)}) collective-permute-start(bf16[2,2,130,256]{3,2,1,0:T(8,128)(2,1)S(1)} %pad_maximum_fusion.1), channel_id=1, source_target_pairs={{4,0},{8,4},{12,8},{16,12},{20,16},{24,20},{28,24},{5,1},{9,5},{13... | collective-permute-start | bytes 798728 | tf_op jit(solution)/shard_map/ppermute | solution.py:20
  17.3 5.1 %encode.7.refs_1_ = bf16[2,6,128,256]{3,2,1,0:T(8,128)(2,1)} custom-call(bf16[2,12,128,256]{3,2,1,0:T(8,128)(2,1)} %image_ref.7, bf16[2,2,12,256]{3,2,1,0:T(8,128)(2,1)} %copy-done.6, bf16[2,2,12,256]{3,2,1,0:T(8,128)(2,1)} %copy-done.7, bf16[3,768,256]{2,1,0:T(8,128)(2,1)} %bitcast.27, f32[1,256]{1,0:T(1,128)} %bitcast.31), custom_call_target="tpu_custom_call" | custom-call | flops 1811939328 | bytes 1572864 | tf_op jit(solution)/shard_map/encode/pallas_call | solution.py:96
  22.4 2.9 %collective-permute-start.7 = (bf16[2,6,128,256]{3,2,1,0:T(8,128)(2,1)}, bf16[2,6,128,256]{3,2,1,0:T(8,128)(2,1)S(1)}, u32[]{:S(2)}, u32[]{:S(2)}) collective-permute-start(bf16[2,6,128,256]{3,2,1,0:T(8,128)(2,1)} %encode.7.refs_1_), channel_id=1, source_target_pairs={{0,1},{1,2},{2,3},{4,5},{5,6},{6,7},{8,9},{9,10},{10,11},{12,13},{... | collective-permute-start | bytes 2359304 | tf_op jit(solution)/shard_map/ppermute | solution.py:20
  25.3 4.6 %encode.6.refs_0_ = bf16[2,6,128,256]{3,2,1,0:T(8,128)(2,1)} custom-call(bf16[2,12,128,256]{3,2,1,0:T(8,128)(2,1)} %image_ref.6, bf16[2,2,12,256]{3,2,1,0:T(8,128)(2,1)} %copy-done.6, bf16[2,2,12,256]{3,2,1,0:T(8,128)(2,1)} %copy-done.7, bf16[3,768,256]{2,1,0:T(8,128)(2,1)} %bitcast.28, f32[1,256]{1,0:T(1,128)} %bitcast.32), custom_call_target="tpu_custom_call" | custom-call | flops 1811939328 | bytes 1572864 | tf_op jit(solution)/shard_map/encode/pallas_call | solution.py:96
  29.9 1.9 %collective-permute-start.8 = (bf16[2,6,128,256]{3,2,1,0:T(8,128)(2,1)}, bf16[2,6,128,256]{3,2,1,0:T(8,128)(2,1)S(1)}, u32[]{:S(2)}, u32[]{:S(2)}) collective-permute-start(bf16[2,6,128,256]{3,2,1,0:T(8,128)(2,1)} %encode.6.refs_0_), channel_id=1, source_target_pairs={{1,0},{2,1},{3,2},{5,4},{6,5},{7,6},{9,8},{10,9},{11,10},{13,12},{... | collective-permute-start | bytes 2359304 | tf_op jit(solution)/shard_map/ppermute | solution.py:20
  33.2 4.6 %encode.4.refs_0_ = bf16[2,6,128,256]{3,2,1,0:T(8,128)(2,1)} custom-call(bf16[2,12,128,256]{3,2,1,0:T(8,128)(2,1)} %image_ref.6, bf16[2,2,12,256]{3,2,1,0:T(8,128)(2,1)} %copy-done.6, bf16[2,2,12,256]{3,2,1,0:T(8,128)(2,1)} %copy-done.7, bf16[2,2,130,256]{3,2,1,0:T(8,128)(2,1)} %copy-done.8, bf16[2,2,130,256]{3,2,1,0:T(8,128)(2,1)} %copy-done.9, ...), custom_call_target="tpu_custom_call" | custom-call | flops 1811939328 | bytes 1572864 | tf_op jit(solution)/shard_map/encode/pallas_call | solution.py:96
  37.8 1.9 %collective-permute-start.5 = (bf16[2,6,128,256]{3,2,1,0:T(8,128)(2,1)}, bf16[2,6,128,256]{3,2,1,0:T(8,128)(2,1)S(1)}, u32[]{:S(2)}, u32[]{:S(2)}) collective-permute-start(bf16[2,6,128,256]{3,2,1,0:T(8,128)(2,1)} %encode.4.refs_0_), channel_id=1, source_target_pairs={{1,0},{2,1},{3,2},{5,4},{6,5},{7,6},{9,8},{10,9},{11,10},{13,12},{... | collective-permute-start | bytes 2359304 | tf_op jit(solution)/shard_map/ppermute | solution.py:20
  39.8 5.2 %encode.5.refs_1_ = bf16[2,6,128,256]{3,2,1,0:T(8,128)(2,1)} custom-call(bf16[2,12,128,256]{3,2,1,0:T(8,128)(2,1)} %image_ref.7, bf16[2,2,12,256]{3,2,1,0:T(8,128)(2,1)} %copy-done.6, bf16[2,2,12,256]{3,2,1,0:T(8,128)(2,1)} %copy-done.7, bf16[2,2,130,256]{3,2,1,0:T(8,128)(2,1)} %copy-done.8, bf16[2,2,130,256]{3,2,1,0:T(8,128)(2,1)} %copy-done.9, ...), custom_call_target="tpu_custom_call" | custom-call | flops 1811939328 | bytes 1572864 | tf_op jit(solution)/shard_map/encode/pallas_call | solution.py:96
  44.9 3.6 %collective-permute-start.4 = (bf16[2,6,128,256]{3,2,1,0:T(8,128)(2,1)}, bf16[2,6,128,256]{3,2,1,0:T(8,128)(2,1)S(1)}, u32[]{:S(2)}, u32[]{:S(2)}) collective-permute-start(bf16[2,6,128,256]{3,2,1,0:T(8,128)(2,1)} %encode.5.refs_1_), channel_id=1, source_target_pairs={{0,1},{1,2},{2,3},{4,5},{5,6},{6,7},{8,9},{9,10},{10,11},{12,13},{... | collective-permute-start | bytes 2359304 | tf_op jit(solution)/shard_map/ppermute | solution.py:20
  50.3 3.7 %triangle.3 = f32[1,6,128,128]{3,2,1,0:T(8,128)} custom-call(bf16[2,6,128,256]{3,2,1,0:T(8,128)(2,1)} %copy-done.2, bf16[2,6,128,256]{3,2,1,0:T(8,128)(2,1)} %copy-done.1), custom_call_target="tpu_custom_call" | custom-call | flops 100663296 | bytes 1572864 | tf_op jit(solution)/shard_map/triangle/pallas_call | solution.py:127
  54.0 2.4 %collective-permute-start.9 = (f32[1,6,128,128]{3,2,1,0:T(8,128)}, f32[1,6,128,128]{3,2,1,0:T(8,128)S(1)}, u32[]{:S(2)}, u32[]{:S(2)}) collective-permute-start(f32[1,6,128,128]{3,2,1,0:T(8,128)} %triangle.3), channel_id=1, source_target_pairs={{0,1},{1,2},{2,3},{4,5},{5,6},{6,7},{8,9},{9,10},{10,11},{12,13},{... | collective-permute-start | bytes 1179656 | tf_op jit(solution)/shard_map/ppermute | solution.py:20
  56.5 1.3 %collective-permute-done.4.right_ref.refs_2_ = bf16[2,6,128,256]{3,2,1,0:T(8,128)(2,1)S(1)} collective-permute-done((bf16[2,6,128,256]{3,2,1,0:T(8,128)(2,1)}, bf16[2,6,128,256]{3,2,1,0:T(8,128)(2,1)S(1)}, u32[]{:S(2)}, u32[]{:S(2)}) %collective-permute-start.4) | collective-permute-done | bytes 786464 | tf_op jit(solution)/shard_map/ppermute | solution.py:20
  58.7 3.7 %triangle.2 = f32[1,6,128,128]{3,2,1,0:T(8,128)} custom-call(bf16[2,6,128,256]{3,2,1,0:T(8,128)(2,1)} %copy-done.3, bf16[2,6,128,256]{3,2,1,0:T(8,128)(2,1)} %copy-done), custom_call_target="tpu_custom_call" | custom-call | flops 100663296 | bytes 1572864 | tf_op jit(solution)/shard_map/triangle/pallas_call | solution.py:127
  62.3 4.3 %collective-permute-start.6 = (f32[1,6,128,128]{3,2,1,0:T(8,128)}, f32[1,6,128,128]{3,2,1,0:T(8,128)S(1)}, u32[]{:S(2)}, u32[]{:S(2)}) collective-permute-start(f32[1,6,128,128]{3,2,1,0:T(8,128)} %triangle.2), channel_id=1, source_target_pairs={{0,1},{1,2},{2,3},{4,5},{5,6},{6,7},{8,9},{9,10},{10,11},{12,13},{... | collective-permute-start | bytes 1179656 | tf_op jit(solution)/shard_map/ppermute | solution.py:20
  67.4 5.2 %volume.2.refs_5_ = f32[2,12,480,128]{3,2,1,0:T(8,128)} custom-call(bf16[2,6,128,256]{3,2,1,0:T(8,128)(2,1)} %encode.6.refs_0_, bf16[2,6,128,256]{3,2,1,0:T(8,128)(2,1)} %encode.7.refs_1_, bf16[2,6,128,256]{3,2,1,0:T(8,128)(2,1)} %copy-done.1, f32[1,6,128,128]{3,2,1,0:T(8,128)} %copy-done.4, bf16[224,256]{1,0:T(8,128)(2,1)} %constant.2.clone.refs_4_), custom_call_target="tpu_custom_call" | custom-call | flops 553648128 | bytes 5308416 | tf_op jit(solution)/shard_map/volume/pallas_call | solution.py:199
  73.4 5.2 %volume.3 = f32[2,12,480,128]{3,2,1,0:T(8,128)} custom-call(bf16[2,6,128,256]{3,2,1,0:T(8,128)(2,1)} %encode.4.refs_0_, bf16[2,6,128,256]{3,2,1,0:T(8,128)(2,1)} %encode.5.refs_1_, bf16[2,6,128,256]{3,2,1,0:T(8,128)(2,1)} %copy-done, f32[1,6,128,128]{3,2,1,0:T(8,128)} %copy-done.5, ...), custom_call_target="tpu_custom_call", output_to_operand_aliasing={{}: (5, {})} | custom-call | flops 553648128 | bytes 5308416 | tf_op jit(solution)/shard_map/volume/pallas_call | solution.py:199
  (36 shorter events, 5.7 us)
Async XLA Ops:
  2.0 7.7 %collective-permute-start = (bf16[2,2,12,256]{3,2,1,0:T(8,128)(2,1)S(1)}, bf16[2,2,12,256]{3,2,1,0:T(8,128)(2,1)S(1)}, u32[]{:S(2)}, u32[]{:S(2)}) collective-permute-start(bf16[2,2,12,256]{3,2,1,0:T(8,128)(2,1)S(1)} %pad_maximum_fusion.2), channel_id=1, source_target_pairs={{0,1},{1,2},{2,3},{4,5},{5,6},{6,7},{8,9},{9,10},{10,11},{12,13},{... | collective-permute-start | bytes 73736 | tf_op jit(solution)/shard_map/ppermute | solution.py:20
  5.8 5.2 %collective-permute-start.1 = (bf16[2,2,12,256]{3,2,1,0:T(8,128)(2,1)S(1)}, bf16[2,2,12,256]{3,2,1,0:T(8,128)(2,1)S(1)}, u32[]{:S(2)}, u32[]{:S(2)}) collective-permute-start(bf16[2,2,12,256]{3,2,1,0:T(8,128)(2,1)S(1)} %pad_maximum_fusion.3), channel_id=1, source_target_pairs={{1,0},{2,1},{3,2},{5,4},{6,5},{7,6},{9,8},{10,9},{11,10},{13,12},{... | collective-permute-start | bytes 73736 | tf_op jit(solution)/shard_map/ppermute | solution.py:20
  9.7 7.6 %copy-start.6 = (bf16[2,2,12,256]{3,2,1,0:T(8,128)(2,1)}, bf16[2,2,12,256]{3,2,1,0:T(8,128)(2,1)S(1)}, u32[]{:S(2)}) copy-start(bf16[2,2,12,256]{3,2,1,0:T(8,128)(2,1)S(1)} %collective-permute-done.before_ref) | copy-start | bytes 73732
  11.0 6.3 %copy-start.7 = (bf16[2,2,12,256]{3,2,1,0:T(8,128)(2,1)}, bf16[2,2,12,256]{3,2,1,0:T(8,128)(2,1)S(1)}, u32[]{:S(2)}) copy-start(bf16[2,2,12,256]{3,2,1,0:T(8,128)(2,1)S(1)} %collective-permute-done.1.after_ref) | copy-start | bytes 73732
  11.0 20.7 %collective-permute-start.2 = (bf16[2,2,130,256]{3,2,1,0:T(8,128)(2,1)S(1)}, bf16[2,2,130,256]{3,2,1,0:T(8,128)(2,1)S(1)}, u32[]{:S(2)}, u32[]{:S(2)}) collective-permute-start(bf16[2,2,130,256]{3,2,1,0:T(8,128)(2,1)S(1)} %pad_maximum_fusion), channel_id=1, source_target_pairs={{0,4},{4,8},{8,12},{12,16},{16,20},{20,24},{24,28},{1,5},{5,9},{9,... | collective-permute-start | bytes 798728 | tf_op jit(solution)/shard_map/ppermute | solution.py:20
  14.2 17.6 %collective-permute-start.3 = (bf16[2,2,130,256]{3,2,1,0:T(8,128)(2,1)S(1)}, bf16[2,2,130,256]{3,2,1,0:T(8,128)(2,1)S(1)}, u32[]{:S(2)}, u32[]{:S(2)}) collective-permute-start(bf16[2,2,130,256]{3,2,1,0:T(8,128)(2,1)S(1)} %pad_maximum_fusion.1), channel_id=1, source_target_pairs={{4,0},{8,4},{12,8},{16,12},{20,16},{24,20},{28,24},{5,1},{9,5},{13... | collective-permute-start | bytes 798728 | tf_op jit(solution)/shard_map/ppermute | solution.py:20
  22.4 26.2 %collective-permute-start.7 = (bf16[2,6,128,256]{3,2,1,0:T(8,128)(2,1)}, bf16[2,6,128,256]{3,2,1,0:T(8,128)(2,1)S(1)}, u32[]{:S(2)}, u32[]{:S(2)}) collective-permute-start(bf16[2,6,128,256]{3,2,1,0:T(8,128)(2,1)} %encode.7.refs_1_), channel_id=1, source_target_pairs={{0,1},{1,2},{2,3},{4,5},{5,6},{6,7},{8,9},{9,10},{10,11},{12,13},{... | collective-permute-start | bytes 2359304 | tf_op jit(solution)/shard_map/ppermute | solution.py:20
  29.9 18.7 %collective-permute-start.8 = (bf16[2,6,128,256]{3,2,1,0:T(8,128)(2,1)}, bf16[2,6,128,256]{3,2,1,0:T(8,128)(2,1)S(1)}, u32[]{:S(2)}, u32[]{:S(2)}) collective-permute-start(bf16[2,6,128,256]{3,2,1,0:T(8,128)(2,1)} %encode.6.refs_0_), channel_id=1, source_target_pairs={{1,0},{2,1},{3,2},{5,4},{6,5},{7,6},{9,8},{10,9},{11,10},{13,12},{... | collective-permute-start | bytes 2359304 | tf_op jit(solution)/shard_map/ppermute | solution.py:20
  31.8 0.7 copy-start.8
  32.5 0.7 copy-start.9
  37.8 18.6 %collective-permute-start.5 = (bf16[2,6,128,256]{3,2,1,0:T(8,128)(2,1)}, bf16[2,6,128,256]{3,2,1,0:T(8,128)(2,1)S(1)}, u32[]{:S(2)}, u32[]{:S(2)}) collective-permute-start(bf16[2,6,128,256]{3,2,1,0:T(8,128)(2,1)} %encode.4.refs_0_), channel_id=1, source_target_pairs={{1,0},{2,1},{3,2},{5,4},{6,5},{7,6},{9,8},{10,9},{11,10},{13,12},{... | collective-permute-start | bytes 2359304 | tf_op jit(solution)/shard_map/ppermute | solution.py:20
  44.9 12.9 %collective-permute-start.4 = (bf16[2,6,128,256]{3,2,1,0:T(8,128)(2,1)}, bf16[2,6,128,256]{3,2,1,0:T(8,128)(2,1)S(1)}, u32[]{:S(2)}, u32[]{:S(2)}) collective-permute-start(bf16[2,6,128,256]{3,2,1,0:T(8,128)(2,1)} %encode.5.refs_1_), channel_id=1, source_target_pairs={{0,1},{1,2},{2,3},{4,5},{5,6},{6,7},{8,9},{9,10},{10,11},{12,13},{... | collective-permute-start | bytes 2359304 | tf_op jit(solution)/shard_map/ppermute | solution.py:20
  48.6 0.9 %copy-start.1 = (bf16[2,6,128,256]{3,2,1,0:T(8,128)(2,1)}, bf16[2,6,128,256]{3,2,1,0:T(8,128)(2,1)S(1)}, u32[]{:S(2)}) copy-start(bf16[2,6,128,256]{3,2,1,0:T(8,128)(2,1)S(1)} %collective-permute-done.7.right_ref.refs_2_) | copy-start | bytes 2359300
  49.4 0.9 %copy-start.2 = (bf16[2,6,128,256]{3,2,1,0:T(8,128)(2,1)}, bf16[2,6,128,256]{3,2,1,0:T(8,128)(2,1)S(1)}, u32[]{:S(2)}) copy-start(bf16[2,6,128,256]{3,2,1,0:T(8,128)(2,1)S(1)} %collective-permute-done.8.left_ref) | copy-start | bytes 2359300
  54.0 12.6 %collective-permute-start.9 = (f32[1,6,128,128]{3,2,1,0:T(8,128)}, f32[1,6,128,128]{3,2,1,0:T(8,128)S(1)}, u32[]{:S(2)}, u32[]{:S(2)}) collective-permute-start(f32[1,6,128,128]{3,2,1,0:T(8,128)} %triangle.3), channel_id=1, source_target_pairs={{0,1},{1,2},{2,3},{4,5},{5,6},{6,7},{8,9},{9,10},{10,11},{12,13},{... | collective-permute-start | bytes 1179656 | tf_op jit(solution)/shard_map/ppermute | solution.py:20
  56.4 1.3 %copy-start.3 = (bf16[2,6,128,256]{3,2,1,0:T(8,128)(2,1)}, bf16[2,6,128,256]{3,2,1,0:T(8,128)(2,1)S(1)}, u32[]{:S(2)}) copy-start(bf16[2,6,128,256]{3,2,1,0:T(8,128)(2,1)S(1)} %collective-permute-done.5.left_ref) | copy-start | bytes 2359300
  57.8 0.9 %copy-start = (bf16[2,6,128,256]{3,2,1,0:T(8,128)(2,1)}, bf16[2,6,128,256]{3,2,1,0:T(8,128)(2,1)S(1)}, u32[]{:S(2)}) copy-start(bf16[2,6,128,256]{3,2,1,0:T(8,128)(2,1)S(1)} %collective-permute-done.4.right_ref.refs_2_) | copy-start | bytes 2359300
  62.3 10.2 %collective-permute-start.6 = (f32[1,6,128,128]{3,2,1,0:T(8,128)}, f32[1,6,128,128]{3,2,1,0:T(8,128)S(1)}, u32[]{:S(2)}, u32[]{:S(2)}) collective-permute-start(f32[1,6,128,128]{3,2,1,0:T(8,128)} %triangle.2), channel_id=1, source_target_pairs={{0,1},{1,2},{2,3},{4,5},{5,6},{6,7},{8,9},{9,10},{10,11},{12,13},{... | collective-permute-start | bytes 1179656 | tf_op jit(solution)/shard_map/ppermute | solution.py:20
  66.6 0.8 copy-start.4
  72.6 0.8 %copy-start.5 = (f32[1,6,128,128]{3,2,1,0:T(8,128)}, f32[1,6,128,128]{3,2,1,0:T(8,128)S(1)}, u32[]{:S(2)}) copy-start(f32[1,6,128,128]{3,2,1,0:T(8,128)S(1)} %collective-permute-done.6.refs_3_) | copy-start | bytes 1179652

commit v3 on v2

--- a/solution.py
+++ b/solution.py
@@ -35,6 +35,9 @@
 
 def dot_t(a, b):
     return lax.dot_general(a, b, (((1,), (1,)), ((), ())), preferred_element_type=F32)
+
+
+FULL = pltpu.CompilerParams(vmem_limit_bytes=67043328)
 
 
 def in_hbm(value):
@@ -106,6 +109,7 @@
         out_specs=pl.BlockSpec((1, count, breadth, channels), lambda b: (b, 0, 0, 0)),
         scratch_shapes=[pltpu.VMEM((len(needed), breadth, 3 * channels), BF16)],
         cost_estimate=cost(batch * count * breadth * channels * channels * 18, 2 * image.size),
+        compiler_params=FULL,
         name="encode",
     )(*operands)
 
@@ -116,13 +120,13 @@
     def kernel(left_ref, right_ref, out_ref):
         near = iota((breadth, breadth), 1) > iota((breadth, breadth), 0)
         flip = reversal(breadth)
-        for i in range(2):
-            for b in range(0, batch, 2):
-                upper = dot_t(left_ref[b, i], right_ref[b, i])
-                upper = pltpu.roll(upper, 1, 1, stride=1, stride_axis=0)
-                turned = dot(flip, left_ref[b + 1, i]).astype(BF16)
-                lower = dot_t(turned, right_ref[b + 1, i])
-                out_ref[b // 2, i] = jnp.where(near, upper, lower)
+        spots = [(b, i) for i in range(2) for b in range(0, batch, 2)]
+        turned = [dot(flip, left_ref[b + 1, i]).astype(BF16) for b, i in spots]
+        upper = [dot_t(left_ref[b, i], right_ref[b, i]) for b, i in spots]
+        lower = [dot_t(t, right_ref[b + 1, i]) for t, (b, i) in zip(turned, spots)]
+        upper = [pltpu.roll(u, 1, 1, stride=1, stride_axis=0) for u in upper]
+        for k, (b, i) in enumerate(spots):
+            out_ref[b // 2, i] = jnp.where(near, upper[k], lower[k])
 
     return pl.pallas_call(
         kernel,
@@ -131,6 +135,7 @@
         in_specs=[pl.BlockSpec((batch, 2, breadth, channels), lambda j: (0, j, 0, 0))] * 2,
         out_specs=pl.BlockSpec((batch // 2, 2, breadth, breadth), lambda j: (0, j, 0, 0)),
         cost_estimate=cost(2 * batch * count * breadth * breadth * channels, 4 * left.size),
+        compiler_params=FULL,
         name="triangle",
     )(in_hbm(left), in_hbm(right))
 
@@ -209,6 +214,7 @@
             2 * batch * count * breadth * DISP * (channels + 2 * pooled),
             batch * count * breadth * (6 * channels + 4 * width),
         ),
+        compiler_params=FULL,
         name="volume",
     )(*operands)
 

time: 79.3 us -> 78.3 us (0.987)
  local copies, waits for them, and re-layouts: 9.6 us -> 4.58 us
  starting transfers between devices: 28.9 us -> 30.4 us
  other arithmetic: 0.07 us -> 1.48 us
  waiting for transfers between devices: 2.62 us -> 3.82 us
    unnamed x20 -> x4, local copies, waits for them, and re-layouts: 5.61 us -> 0.59 us
    ppermute x10, starting transfers between devices: 28.9 us -> 30.4 us  [shifted(): lax.ppermute(value, axis, [(i, i + steps) for i in range(first, last)])]
    concatenate x2, other arithmetic: 0.05 us -> 1.46 us  [edge(): return jnp.concatenate(parts, axis=2)]
    ppermute x10, waiting for transfers between devices: 2.62 us -> 3.82 us  [shifted(): lax.ppermute(value, axis, [(i, i + steps) for i in range(first, last)])]
  transfers between devices with their start and end apart: 10 -> 10, of which waited for: 2 -> 2; matrix products, arithmetic and copies ran while one was open for 3% -> 4% of each run, Pallas kernels for 41% -> 41%
where the time goes in v3:
time: 78.3 us; the launch traced here: 77 us
  Pallas kernels  36.5 us (47%)
  starting transfers between devices  30.4 us (39%)
  local copies, waits for them, and re-layouts  4.58 us (6%)
  waiting for transfers between devices  3.82 us (5%)
  other arithmetic  1.48 us (2%)
    ppermute x10, starting transfers between devices, shifted(): lax.ppermute(value, axis, [(i, i + steps) for i in range(first, last)])  30.4 us
    pallas_call x4, Pallas kernels, encode(): pl.pallas_call(kernel, grid=(batch,), out_shape=jax.ShapeDtypeStruct((bat...  19.4 us
    pallas_call x2, Pallas kernels, volume(): pl.pallas_call(kernel, grid=(count // 2,), out_shape=jax.ShapeDtypeStruct...  10.4 us
    pallas_call x2, Pallas kernels, triangle(): pl.pallas_call(kernel, grid=(count // 2,), out_shape=jax.ShapeDtypeStruct...  6.74 us
    ppermute x10, waiting for transfers between devices, shifted(): lax.ppermute(value, axis, [(i, i + steps) for i in range(first, last)])  3.82 us
    another operation x2, local copies, waits for them, and re-layouts, edge(): parts = [jnp.stack([f[:, row] for f in both])]  1.99 us
    slice x2, local copies, waits for them, and re-layouts, shards(): f[:, :, 0]  1.97 us
  transfers between devices with their start and end apart: 10, of which 2 were waited for; matrix products, arithmetic and copies ran while one was open for 4% of the time, Pallas kernels for 41%

profile of v3, /device:TPU:25, one launch (start us, length us, event | category | flops | bytes accessed | tf_op | source)
XLA Modules:
  0.0 77.0 jit_solution(7333056701638057436)
XLA Ops:
  0.0 1.0 %fusion.1 = (bf16[2,12,1,256]{3,2,1,0:T(2,128)(2,1)S(1)}, bf16[2,12,1,256]{3,2,1,0:T(2,128)(2,1)S(1)}) fusion(bf16[2,12,128,256]{3,2,1,0:T(8,128)(2,1)} %image_ref.6), kind=kLoop, calls=%fused_computation.13 | loop fusion | bytes 49152 | tf_op jit(solution)/shard_map/slice | solution.py:228
  1.0 1.0 %fusion = (bf16[2,12,1,256]{3,2,1,0:T(2,128)(2,1)S(1)}, bf16[2,12,1,256]{3,2,1,0:T(2,128)(2,1)S(1)}) fusion(bf16[2,12,128,256]{3,2,1,0:T(8,128)(2,1)} %image_ref.7), kind=kLoop, calls=%fused_computation.12 | loop fusion | bytes 49152 | tf_op jit(solution)/shard_map/slice | solution.py:228
  2.0 3.7 %collective-permute-start = (bf16[2,2,12,256]{3,2,1,0:T(8,128)(2,1)S(1)}, bf16[2,2,12,256]{3,2,1,0:T(8,128)(2,1)S(1)}, u32[]{:S(2)}, u32[]{:S(2)}) collective-permute-start(bf16[2,2,12,256]{3,2,1,0:T(8,128)(2,1)S(1)} %pad_maximum_fusion.2), channel_id=1, source_target_pairs={{0,1},{1,2},{2,3},{4,5},{5,6},{6,7},{8,9},{9,10},{10,11},{12,13},{... | collective-permute-start | bytes 73736 | tf_op jit(solution)/shard_map/ppermute | solution.py:20
  5.8 1.9 %collective-permute-start.1 = (bf16[2,2,12,256]{3,2,1,0:T(8,128)(2,1)S(1)}, bf16[2,2,12,256]{3,2,1,0:T(8,128)(2,1)S(1)}, u32[]{:S(2)}, u32[]{:S(2)}) collective-permute-start(bf16[2,2,12,256]{3,2,1,0:T(8,128)(2,1)S(1)} %pad_maximum_fusion.3), channel_id=1, source_target_pairs={{1,0},{2,1},{3,2},{5,4},{6,5},{7,6},{9,8},{10,9},{11,10},{13,12},{... | collective-permute-start | bytes 73736 | tf_op jit(solution)/shard_map/ppermute | solution.py:20
  7.7 1.0 %slice_bitcast_fusion = (bf16[1,2,128,256]{3,2,1,0:T(8,128)(2,1)S(1)}, bf16[1,2,128,256]{3,2,1,0:T(8,128)(2,1)S(1)}) fusion(bf16[2,12,128,256]{3,2,1,0:T(8,128)(2,1)} %image_ref.6), kind=kLoop, calls=%fused_computation.2 | loop fusion | bytes 524288 | tf_op jit(solution)/shard_map/stack;squeeze | solution.py:232
  8.7 1.0 %slice_bitcast_fusion.1 = (bf16[1,2,128,256]{3,2,1,0:T(8,128)(2,1)S(1)}, bf16[1,2,128,256]{3,2,1,0:T(8,128)(2,1)S(1)}) fusion(bf16[2,12,128,256]{3,2,1,0:T(8,128)(2,1)} %image_ref.7), kind=kLoop, calls=%fused_computation.3 | loop fusion | bytes 524288 | tf_op jit(solution)/shard_map/stack;squeeze | solution.py:232
  9.7 1.3 %collective-permute-done.1.after_ref = bf16[2,2,12,256]{3,2,1,0:T(8,128)(2,1)S(1)} collective-permute-done((bf16[2,2,12,256]{3,2,1,0:T(8,128)(2,1)S(1)}, bf16[2,2,12,256]{3,2,1,0:T(8,128)(2,1)S(1)}, u32[]{:S(2)}, u32[]{:S(2)}) %collective-permute-start.1) | collective-permute-done | bytes 24608 | tf_op jit(solution)/shard_map/ppermute | solution.py:20
  12.3 3.1 %collective-permute-start.2 = (bf16[2,2,130,256]{3,2,1,0:T(8,128)(2,1)}, bf16[2,2,130,256]{3,2,1,0:T(8,128)(2,1)}, u32[]{:S(2)}, u32[]{:S(2)}) collective-permute-start(bf16[2,2,130,256]{3,2,1,0:T(8,128)(2,1)} %pad_maximum_fusion), channel_id=1, source_target_pairs={{0,4},{4,8},{8,12},{12,16},{16,20},{20,24},{24,28},{1,5},{5,9},{9,... | collective-permute-start | bytes 798728 | tf_op jit(solution)/shard_map/ppermute | solution.py:20
  16.2 3.1 %collective-permute-start.3 = (bf16[2,2,130,256]{3,2,1,0:T(8,128)(2,1)}, bf16[2,2,130,256]{3,2,1,0:T(8,128)(2,1)}, u32[]{:S(2)}, u32[]{:S(2)}) collective-permute-start(bf16[2,2,130,256]{3,2,1,0:T(8,128)(2,1)} %pad_maximum_fusion.1), channel_id=1, source_target_pairs={{4,0},{8,4},{12,8},{16,12},{20,16},{24,20},{28,24},{5,1},{9,5},{13... | collective-permute-start | bytes 798728 | tf_op jit(solution)/shard_map/ppermute | solution.py:20
  19.2 5.1 %encode.7.refs_1_ = bf16[2,6,128,256]{3,2,1,0:T(8,128)(2,1)} custom-call(bf16[2,12,128,256]{3,2,1,0:T(8,128)(2,1)} %image_ref.7, bf16[2,2,12,256]{3,2,1,0:T(8,128)(2,1)} %copy-done, bf16[2,2,12,256]{3,2,1,0:T(8,128)(2,1)} %copy-done.1, bf16[3,768,256]{2,1,0:T(8,128)(2,1)} %bitcast.27, f32[1,256]{1,0:T(1,128)} %bitcast.31), custom_call_target="tpu_custom_call" | custom-call | flops 1811939328 | bytes 1572864 | tf_op jit(solution)/shard_map/encode/pallas_call | solution.py:99
  24.3 3.5 %collective-permute-start.7 = (bf16[2,6,128,256]{3,2,1,0:T(8,128)(2,1)}, bf16[2,6,128,256]{3,2,1,0:T(8,128)(2,1)}, u32[]{:S(2)}, u32[]{:S(2)}) collective-permute-start(bf16[2,6,128,256]{3,2,1,0:T(8,128)(2,1)} %encode.7.refs_1_), channel_id=1, source_target_pairs={{0,1},{1,2},{2,3},{4,5},{5,6},{6,7},{8,9},{9,10},{10,11},{12,13},{... | collective-permute-start | bytes 2359304 | tf_op jit(solution)/shard_map/ppermute | solution.py:20
  27.8 4.5 %encode.6.refs_0_ = bf16[2,6,128,256]{3,2,1,0:T(8,128)(2,1)} custom-call(bf16[2,12,128,256]{3,2,1,0:T(8,128)(2,1)} %image_ref.6, bf16[2,2,12,256]{3,2,1,0:T(8,128)(2,1)} %copy-done, bf16[2,2,12,256]{3,2,1,0:T(8,128)(2,1)} %copy-done.1, bf16[3,768,256]{2,1,0:T(8,128)(2,1)} %bitcast.28, f32[1,256]{1,0:T(1,128)} %bitcast.32), custom_call_target="tpu_custom_call" | custom-call | flops 1811939328 | bytes 1572864 | tf_op jit(solution)/shard_map/encode/pallas_call | solution.py:99
  32.4 1.9 %collective-permute-start.8 = (bf16[2,6,128,256]{3,2,1,0:T(8,128)(2,1)}, bf16[2,6,128,256]{3,2,1,0:T(8,128)(2,1)}, u32[]{:S(2)}, u32[]{:S(2)}) collective-permute-start(bf16[2,6,128,256]{3,2,1,0:T(8,128)(2,1)} %encode.6.refs_0_), channel_id=1, source_target_pairs={{1,0},{2,1},{3,2},{5,4},{6,5},{7,6},{9,8},{10,9},{11,10},{13,12},{... | collective-permute-start | bytes 2359304 | tf_op jit(solution)/shard_map/ppermute | solution.py:20
  34.3 4.6 %encode.4.refs_0_ = bf16[2,6,128,256]{3,2,1,0:T(8,128)(2,1)} custom-call(bf16[2,12,128,256]{3,2,1,0:T(8,128)(2,1)} %image_ref.6, bf16[2,2,12,256]{3,2,1,0:T(8,128)(2,1)} %copy-done, bf16[2,2,12,256]{3,2,1,0:T(8,128)(2,1)} %copy-done.1, bf16[2,2,130,256]{3,2,1,0:T(8,128)(2,1)} %collective-permute-done.2.rest_0_, ...), custom_call_target="tpu_custom_call" | custom-call | flops 1811939328 | bytes 1572864 | tf_op jit(solution)/shard_map/encode/pallas_call | solution.py:99
  38.9 1.9 %collective-permute-start.5 = (bf16[2,6,128,256]{3,2,1,0:T(8,128)(2,1)}, bf16[2,6,128,256]{3,2,1,0:T(8,128)(2,1)}, u32[]{:S(2)}, u32[]{:S(2)}) collective-permute-start(bf16[2,6,128,256]{3,2,1,0:T(8,128)(2,1)} %encode.4.refs_0_), channel_id=1, source_target_pairs={{1,0},{2,1},{3,2},{5,4},{6,5},{7,6},{9,8},{10,9},{11,10},{13,12},{... | collective-permute-start | bytes 2359304 | tf_op jit(solution)/shard_map/ppermute | solution.py:20
  40.8 5.1 %encode.5.refs_1_ = bf16[2,6,128,256]{3,2,1,0:T(8,128)(2,1)} custom-call(bf16[2,12,128,256]{3,2,1,0:T(8,128)(2,1)} %image_ref.7, bf16[2,2,12,256]{3,2,1,0:T(8,128)(2,1)} %copy-done, bf16[2,2,12,256]{3,2,1,0:T(8,128)(2,1)} %copy-done.1, bf16[2,2,130,256]{3,2,1,0:T(8,128)(2,1)} %collective-permute-done.2.rest_0_, ...), custom_call_target="tpu_custom_call" | custom-call | flops 1811939328 | bytes 1572864 | tf_op jit(solution)/shard_map/encode/pallas_call | solution.py:99
  46.0 3.6 %collective-permute-start.4 = (bf16[2,6,128,256]{3,2,1,0:T(8,128)(2,1)}, bf16[2,6,128,256]{3,2,1,0:T(8,128)(2,1)}, u32[]{:S(2)}, u32[]{:S(2)}) collective-permute-start(bf16[2,6,128,256]{3,2,1,0:T(8,128)(2,1)} %encode.5.refs_1_), channel_id=1, source_target_pairs={{0,1},{1,2},{2,3},{4,5},{5,6},{6,7},{8,9},{9,10},{10,11},{12,13},{... | collective-permute-start | bytes 2359304 | tf_op jit(solution)/shard_map/ppermute | solution.py:20
  49.7 3.4 %triangle.3 = f32[1,6,128,128]{3,2,1,0:T(8,128)} custom-call(bf16[2,6,128,256]{3,2,1,0:T(8,128)(2,1)} %collective-permute-done.8.left_ref, bf16[2,6,128,256]{3,2,1,0:T(8,128)(2,1)} %collective-permute-done.7.right_ref.refs_2_), custom_call_target="tpu_custom_call" | custom-call | flops 100663296 | bytes 1572864 | tf_op jit(solution)/shard_map/triangle/pallas_call | solution.py:131
  53.0 3.3 %collective-permute-start.9 = (f32[1,6,128,128]{3,2,1,0:T(8,128)}, f32[1,6,128,128]{3,2,1,0:T(8,128)}, u32[]{:S(2)}, u32[]{:S(2)}) collective-permute-start(f32[1,6,128,128]{3,2,1,0:T(8,128)} %triangle.3), channel_id=1, source_target_pairs={{0,1},{1,2},{2,3},{4,5},{5,6},{6,7},{8,9},{9,10},{10,11},{12,13},{... | collective-permute-start | bytes 1179656 | tf_op jit(solution)/shard_map/ppermute | solution.py:20
  56.3 2.5 %collective-permute-done.4.right_ref.refs_2_ = bf16[2,6,128,256]{3,2,1,0:T(8,128)(2,1)} collective-permute-done((bf16[2,6,128,256]{3,2,1,0:T(8,128)(2,1)}, bf16[2,6,128,256]{3,2,1,0:T(8,128)(2,1)}, u32[]{:S(2)}, u32[]{:S(2)}) %collective-permute-start.4) | collective-permute-done | bytes 786464 | tf_op jit(solution)/shard_map/ppermute | solution.py:20
  58.9 3.4 %triangle.2 = f32[1,6,128,128]{3,2,1,0:T(8,128)} custom-call(bf16[2,6,128,256]{3,2,1,0:T(8,128)(2,1)} %collective-permute-done.5.left_ref, bf16[2,6,128,256]{3,2,1,0:T(8,128)(2,1)} %collective-permute-done.4.right_ref.refs_2_), custom_call_target="tpu_custom_call" | custom-call | flops 100663296 | bytes 1572864 | tf_op jit(solution)/shard_map/triangle/pallas_call | solution.py:131
  62.2 4.4 %collective-permute-start.6 = (f32[1,6,128,128]{3,2,1,0:T(8,128)}, f32[1,6,128,128]{3,2,1,0:T(8,128)}, u32[]{:S(2)}, u32[]{:S(2)}) collective-permute-start(f32[1,6,128,128]{3,2,1,0:T(8,128)} %triangle.2), channel_id=1, source_target_pairs={{0,1},{1,2},{2,3},{4,5},{5,6},{6,7},{8,9},{9,10},{10,11},{12,13},{... | collective-permute-start | bytes 1179656 | tf_op jit(solution)/shard_map/ppermute | solution.py:20
  66.6 5.2 %volume.2.refs_5_ = f32[2,12,480,128]{3,2,1,0:T(8,128)} custom-call(bf16[2,6,128,256]{3,2,1,0:T(8,128)(2,1)} %encode.6.refs_0_, bf16[2,6,128,256]{3,2,1,0:T(8,128)(2,1)} %encode.7.refs_1_, bf16[2,6,128,256]{3,2,1,0:T(8,128)(2,1)} %collective-permute-done.7.right_ref.refs_2_, f32[1,6,128,128]{3,2,1,0:T(8,128)} %collective-permute-done.9.refs_3_, ...), custom_call_target="tpu_custom_call" | custom-call | flops 553648128 | bytes 5308416 | tf_op jit(solution)/shard_map/volume/pallas_call | solution.py:204
  71.8 5.2 %volume.3 = f32[2,12,480,128]{3,2,1,0:T(8,128)} custom-call(bf16[2,6,128,256]{3,2,1,0:T(8,128)(2,1)} %encode.4.refs_0_, bf16[2,6,128,256]{3,2,1,0:T(8,128)(2,1)} %encode.5.refs_1_, bf16[2,6,128,256]{3,2,1,0:T(8,128)(2,1)} %collective-permute-done.4.right_ref.refs_2_, ...), custom_call_target="tpu_custom_call", output_to_operand_aliasing={{}: (5, {})} | custom-call | flops 553648128 | bytes 5308416 | tf_op jit(solution)/shard_map/volume/pallas_call | solution.py:204
  (20 shorter events, 2.1 us)
Async XLA Ops:
  2.0 7.7 %collective-permute-start = (bf16[2,2,12,256]{3,2,1,0:T(8,128)(2,1)S(1)}, bf16[2,2,12,256]{3,2,1,0:T(8,128)(2,1)S(1)}, u32[]{:S(2)}, u32[]{:S(2)}) collective-permute-start(bf16[2,2,12,256]{3,2,1,0:T(8,128)(2,1)S(1)} %pad_maximum_fusion.2), channel_id=1, source_target_pairs={{0,1},{1,2},{2,3},{4,5},{5,6},{6,7},{8,9},{9,10},{10,11},{12,13},{... | collective-permute-start | bytes 73736 | tf_op jit(solution)/shard_map/ppermute | solution.py:20
  5.8 5.2 %collective-permute-start.1 = (bf16[2,2,12,256]{3,2,1,0:T(8,128)(2,1)S(1)}, bf16[2,2,12,256]{3,2,1,0:T(8,128)(2,1)S(1)}, u32[]{:S(2)}, u32[]{:S(2)}) collective-permute-start(bf16[2,2,12,256]{3,2,1,0:T(8,128)(2,1)S(1)} %pad_maximum_fusion.3), channel_id=1, source_target_pairs={{1,0},{2,1},{3,2},{5,4},{6,5},{7,6},{9,8},{10,9},{11,10},{13,12},{... | collective-permute-start | bytes 73736 | tf_op jit(solution)/shard_map/ppermute | solution.py:20
  9.7 1.3 %copy-start = (bf16[2,2,12,256]{3,2,1,0:T(8,128)(2,1)}, bf16[2,2,12,256]{3,2,1,0:T(8,128)(2,1)S(1)}, u32[]{:S(2)}) copy-start(bf16[2,2,12,256]{3,2,1,0:T(8,128)(2,1)S(1)} %collective-permute-done.before_ref) | copy-start | bytes 73732
  11.0 0.6 copy-start.1
  12.3 21.9 %collective-permute-start.2 = (bf16[2,2,130,256]{3,2,1,0:T(8,128)(2,1)}, bf16[2,2,130,256]{3,2,1,0:T(8,128)(2,1)}, u32[]{:S(2)}, u32[]{:S(2)}) collective-permute-start(bf16[2,2,130,256]{3,2,1,0:T(8,128)(2,1)} %pad_maximum_fusion), channel_id=1, source_target_pairs={{0,4},{4,8},{8,12},{12,16},{16,20},{20,24},{24,28},{1,5},{5,9},{9,... | collective-permute-start | bytes 798728 | tf_op jit(solution)/shard_map/ppermute | solution.py:20
  16.2 18.1 %collective-permute-start.3 = (bf16[2,2,130,256]{3,2,1,0:T(8,128)(2,1)}, bf16[2,2,130,256]{3,2,1,0:T(8,128)(2,1)}, u32[]{:S(2)}, u32[]{:S(2)}) collective-permute-start(bf16[2,2,130,256]{3,2,1,0:T(8,128)(2,1)} %pad_maximum_fusion.1), channel_id=1, source_target_pairs={{4,0},{8,4},{12,8},{16,12},{20,16},{24,20},{28,24},{5,1},{9,5},{13... | collective-permute-start | bytes 798728 | tf_op jit(solution)/shard_map/ppermute | solution.py:20
  24.3 25.3 %collective-permute-start.7 = (bf16[2,6,128,256]{3,2,1,0:T(8,128)(2,1)}, bf16[2,6,128,256]{3,2,1,0:T(8,128)(2,1)}, u32[]{:S(2)}, u32[]{:S(2)}) collective-permute-start(bf16[2,6,128,256]{3,2,1,0:T(8,128)(2,1)} %encode.7.refs_1_), channel_id=1, source_target_pairs={{0,1},{1,2},{2,3},{4,5},{5,6},{6,7},{8,9},{9,10},{10,11},{12,13},{... | collective-permute-start | bytes 2359304 | tf_op jit(solution)/shard_map/ppermute | solution.py:20
  32.4 17.3 %collective-permute-start.8 = (bf16[2,6,128,256]{3,2,1,0:T(8,128)(2,1)}, bf16[2,6,128,256]{3,2,1,0:T(8,128)(2,1)}, u32[]{:S(2)}, u32[]{:S(2)}) collective-permute-start(bf16[2,6,128,256]{3,2,1,0:T(8,128)(2,1)} %encode.6.refs_0_), channel_id=1, source_target_pairs={{1,0},{2,1},{3,2},{5,4},{6,5},{7,6},{9,8},{10,9},{11,10},{13,12},{... | collective-permute-start | bytes 2359304 | tf_op jit(solution)/shard_map/ppermute | solution.py:20
  38.9 17.4 %collective-permute-start.5 = (bf16[2,6,128,256]{3,2,1,0:T(8,128)(2,1)}, bf16[2,6,128,256]{3,2,1,0:T(8,128)(2,1)}, u32[]{:S(2)}, u32[]{:S(2)}) collective-permute-start(bf16[2,6,128,256]{3,2,1,0:T(8,128)(2,1)} %encode.4.refs_0_), channel_id=1, source_target_pairs={{1,0},{2,1},{3,2},{5,4},{6,5},{7,6},{9,8},{10,9},{11,10},{13,12},{... | collective-permute-start | bytes 2359304 | tf_op jit(solution)/shard_map/ppermute | solution.py:20
  46.0 12.9 %collective-permute-start.4 = (bf16[2,6,128,256]{3,2,1,0:T(8,128)(2,1)}, bf16[2,6,128,256]{3,2,1,0:T(8,128)(2,1)}, u32[]{:S(2)}, u32[]{:S(2)}) collective-permute-start(bf16[2,6,128,256]{3,2,1,0:T(8,128)(2,1)} %encode.5.refs_1_), channel_id=1, source_target_pairs={{0,1},{1,2},{2,3},{4,5},{5,6},{6,7},{8,9},{9,10},{10,11},{12,13},{... | collective-permute-start | bytes 2359304 | tf_op jit(solution)/shard_map/ppermute | solution.py:20
  53.0 13.6 %collective-permute-start.9 = (f32[1,6,128,128]{3,2,1,0:T(8,128)}, f32[1,6,128,128]{3,2,1,0:T(8,128)}, u32[]{:S(2)}, u32[]{:S(2)}) collective-permute-start(f32[1,6,128,128]{3,2,1,0:T(8,128)} %triangle.3), channel_id=1, source_target_pairs={{0,1},{1,2},{2,3},{4,5},{5,6},{6,7},{8,9},{9,10},{10,11},{12,13},{... | collective-permute-start | bytes 1179656 | tf_op jit(solution)/shard_map/ppermute | solution.py:20
  62.2 9.6 %collective-permute-start.6 = (f32[1,6,128,128]{3,2,1,0:T(8,128)}, f32[1,6,128,128]{3,2,1,0:T(8,128)}, u32[]{:S(2)}, u32[]{:S(2)}) collective-permute-start(f32[1,6,128,128]{3,2,1,0:T(8,128)} %triangle.2), channel_id=1, source_target_pairs={{0,1},{1,2},{2,3},{4,5},{5,6},{6,7},{8,9},{9,10},{10,11},{12,13},{... | collective-permute-start | bytes 1179656 | tf_op jit(solution)/shard_map/ppermute | solution.py:20

commit v4 on v3

--- a/solution.py
+++ b/solution.py
@@ -109,7 +109,7 @@
         out_specs=pl.BlockSpec((1, count, breadth, channels), lambda b: (b, 0, 0, 0)),
         scratch_shapes=[pltpu.VMEM((len(needed), breadth, 3 * channels), BF16)],
         cost_estimate=cost(batch * count * breadth * channels * channels * 18, 2 * image.size),
-        compiler_params=FULL,
+        compiler_params=None if edges is None else FULL,
         name="encode",
     )(*operands)
 

time: 78.3 us -> 76.8 us (0.981)
  other arithmetic: 1.48 us -> 0.07 us
    concatenate x2, other arithmetic: 1.46 us -> 0.05 us  [edge(): return jnp.concatenate(parts, axis=2)]
  transfers between devices with their start and end apart: 10 -> 10, of which waited for: 2 -> 2; matrix products, arithmetic and copies ran while one was open for 4% -> 3% of each run, Pallas kernels for 41% -> 41%
where the time goes in v4:
time: 76.8 us; the launch traced here: 75.6 us
  Pallas kernels  36.6 us (48%)
  starting transfers between devices  29.9 us (39%)
  local copies, waits for them, and re-layouts  4.7 us (6%)
  waiting for transfers between devices  4.16 us (5%)
    ppermute x10, starting transfers between devices, shifted(): lax.ppermute(value, axis, [(i, i + steps) for i in range(first, last)])  29.9 us
    pallas_call x4, Pallas kernels, encode(): pl.pallas_call(kernel, grid=(batch,), out_shape=jax.ShapeDtypeStruct((bat...  19.4 us
    pallas_call x2, Pallas kernels, volume(): pl.pallas_call(kernel, grid=(count // 2,), out_shape=jax.ShapeDtypeStruct...  10.4 us
    pallas_call x2, Pallas kernels, triangle(): pl.pallas_call(kernel, grid=(count // 2,), out_shape=jax.ShapeDtypeStruct...  6.76 us
    ppermute x10, waiting for transfers between devices, shifted(): lax.ppermute(value, axis, [(i, i + steps) for i in range(first, last)])  4.16 us
    another operation x2, local copies, waits for them, and re-layouts, edge(): parts = [jnp.stack([f[:, row] for f in both])]  1.99 us
    slice x2, local copies, waits for them, and re-layouts, shards(): f[:, :, 0]  1.97 us
  transfers between devices with their start and end apart: 10, of which 2 were waited for; matrix products, arithmetic and copies ran while one was open for 3% of the time, Pallas kernels for 41%

profile of v4, /device:TPU:25, one launch (start us, length us, event | category | flops | bytes accessed | tf_op | source)
XLA Modules:
  0.0 75.6 jit_solution(14002648582596029184)
XLA Ops:
  0.0 1.0 %fusion.1 = (bf16[2,12,1,256]{3,2,1,0:T(2,128)(2,1)S(1)}, bf16[2,12,1,256]{3,2,1,0:T(2,128)(2,1)S(1)}) fusion(bf16[2,12,128,256]{3,2,1,0:T(8,128)(2,1)} %image_ref.6), kind=kLoop, calls=%fused_computation.13 | loop fusion | bytes 49152 | tf_op jit(solution)/shard_map/slice | solution.py:228
  1.0 1.0 %fusion = (bf16[2,12,1,256]{3,2,1,0:T(2,128)(2,1)S(1)}, bf16[2,12,1,256]{3,2,1,0:T(2,128)(2,1)S(1)}) fusion(bf16[2,12,128,256]{3,2,1,0:T(8,128)(2,1)} %image_ref.7), kind=kLoop, calls=%fused_computation.12 | loop fusion | bytes 49152 | tf_op jit(solution)/shard_map/slice | solution.py:228
  2.0 3.7 %collective-permute-start = (bf16[2,2,12,256]{3,2,1,0:T(8,128)(2,1)S(1)}, bf16[2,2,12,256]{3,2,1,0:T(8,128)(2,1)S(1)}, u32[]{:S(2)}, u32[]{:S(2)}) collective-permute-start(bf16[2,2,12,256]{3,2,1,0:T(8,128)(2,1)S(1)} %pad_maximum_fusion.2), channel_id=1, source_target_pairs={{0,1},{1,2},{2,3},{4,5},{5,6},{6,7},{8,9},{9,10},{10,11},{12,13},{... | collective-permute-start | bytes 73736 | tf_op jit(solution)/shard_map/ppermute | solution.py:20
  5.8 1.9 %collective-permute-start.1 = (bf16[2,2,12,256]{3,2,1,0:T(8,128)(2,1)S(1)}, bf16[2,2,12,256]{3,2,1,0:T(8,128)(2,1)S(1)}, u32[]{:S(2)}, u32[]{:S(2)}) collective-permute-start(bf16[2,2,12,256]{3,2,1,0:T(8,128)(2,1)S(1)} %pad_maximum_fusion.3), channel_id=1, source_target_pairs={{1,0},{2,1},{3,2},{5,4},{6,5},{7,6},{9,8},{10,9},{11,10},{13,12},{... | collective-permute-start | bytes 73736 | tf_op jit(solution)/shard_map/ppermute | solution.py:20
  7.7 1.0 %slice_bitcast_fusion = (bf16[1,2,128,256]{3,2,1,0:T(8,128)(2,1)S(1)}, bf16[1,2,128,256]{3,2,1,0:T(8,128)(2,1)S(1)}) fusion(bf16[2,12,128,256]{3,2,1,0:T(8,128)(2,1)} %image_ref.6), kind=kLoop, calls=%fused_computation.2 | loop fusion | bytes 524288 | tf_op jit(solution)/shard_map/stack;squeeze | solution.py:232
  8.7 1.0 %slice_bitcast_fusion.1 = (bf16[1,2,128,256]{3,2,1,0:T(8,128)(2,1)S(1)}, bf16[1,2,128,256]{3,2,1,0:T(8,128)(2,1)S(1)}) fusion(bf16[2,12,128,256]{3,2,1,0:T(8,128)(2,1)} %image_ref.7), kind=kLoop, calls=%fused_computation.3 | loop fusion | bytes 524288 | tf_op jit(solution)/shard_map/stack;squeeze | solution.py:232
  9.7 1.3 %collective-permute-done.1.after_ref = bf16[2,2,12,256]{3,2,1,0:T(8,128)(2,1)S(1)} collective-permute-done((bf16[2,2,12,256]{3,2,1,0:T(8,128)(2,1)S(1)}, bf16[2,2,12,256]{3,2,1,0:T(8,128)(2,1)S(1)}, u32[]{:S(2)}, u32[]{:S(2)}) %collective-permute-start.1) | collective-permute-done | bytes 24608 | tf_op jit(solution)/shard_map/ppermute | solution.py:20
  11.0 3.1 %collective-permute-start.2 = (bf16[2,2,130,256]{3,2,1,0:T(8,128)(2,1)S(1)}, bf16[2,2,130,256]{3,2,1,0:T(8,128)(2,1)S(1)}, u32[]{:S(2)}, u32[]{:S(2)}) collective-permute-start(bf16[2,2,130,256]{3,2,1,0:T(8,128)(2,1)S(1)} %pad_maximum_fusion), channel_id=1, source_target_pairs={{0,4},{4,8},{8,12},{12,16},{16,20},{20,24},{24,28},{1,5},{5,9},{9,... | collective-permute-start | bytes 798728 | tf_op jit(solution)/shard_map/ppermute | solution.py:20
  14.2 3.1 %collective-permute-start.3 = (bf16[2,2,130,256]{3,2,1,0:T(8,128)(2,1)S(1)}, bf16[2,2,130,256]{3,2,1,0:T(8,128)(2,1)}, u32[]{:S(2)}, u32[]{:S(2)}) collective-permute-start(bf16[2,2,130,256]{3,2,1,0:T(8,128)(2,1)S(1)} %pad_maximum_fusion.1), channel_id=1, source_target_pairs={{4,0},{8,4},{12,8},{16,12},{20,16},{24,20},{28,24},{5,1},{9,5},{13... | collective-permute-start | bytes 798728 | tf_op jit(solution)/shard_map/ppermute | solution.py:20
  17.3 5.1 %encode.7.refs_1_ = bf16[2,6,128,256]{3,2,1,0:T(8,128)(2,1)} custom-call(bf16[2,12,128,256]{3,2,1,0:T(8,128)(2,1)} %image_ref.7, bf16[2,2,12,256]{3,2,1,0:T(8,128)(2,1)} %copy-done, bf16[2,2,12,256]{3,2,1,0:T(8,128)(2,1)} %copy-done.1, bf16[3,768,256]{2,1,0:T(8,128)(2,1)} %bitcast.27, f32[1,256]{1,0:T(1,128)} %bitcast.31), custom_call_target="tpu_custom_call" | custom-call | flops 1811939328 | bytes 1572864 | tf_op jit(solution)/shard_map/encode/pallas_call | solution.py:99
  22.4 2.9 %collective-permute-start.7 = (bf16[2,6,128,256]{3,2,1,0:T(8,128)(2,1)}, bf16[2,6,128,256]{3,2,1,0:T(8,128)(2,1)}, u32[]{:S(2)}, u32[]{:S(2)}) collective-permute-start(bf16[2,6,128,256]{3,2,1,0:T(8,128)(2,1)} %encode.7.refs_1_), channel_id=1, source_target_pairs={{0,1},{1,2},{2,3},{4,5},{5,6},{6,7},{8,9},{9,10},{10,11},{12,13},{... | collective-permute-start | bytes 2359304 | tf_op jit(solution)/shard_map/ppermute | solution.py:20
  25.3 4.5 %encode.6.refs_0_ = bf16[2,6,128,256]{3,2,1,0:T(8,128)(2,1)} custom-call(bf16[2,12,128,256]{3,2,1,0:T(8,128)(2,1)} %image_ref.6, bf16[2,2,12,256]{3,2,1,0:T(8,128)(2,1)} %copy-done, bf16[2,2,12,256]{3,2,1,0:T(8,128)(2,1)} %copy-done.1, bf16[3,768,256]{2,1,0:T(8,128)(2,1)} %bitcast.28, f32[1,256]{1,0:T(1,128)} %bitcast.32), custom_call_target="tpu_custom_call" | custom-call | flops 1811939328 | bytes 1572864 | tf_op jit(solution)/shard_map/encode/pallas_call | solution.py:99
  29.9 2.2 %collective-permute-start.8 = (bf16[2,6,128,256]{3,2,1,0:T(8,128)(2,1)}, bf16[2,6,128,256]{3,2,1,0:T(8,128)(2,1)}, u32[]{:S(2)}, u32[]{:S(2)}) collective-permute-start(bf16[2,6,128,256]{3,2,1,0:T(8,128)(2,1)} %encode.6.refs_0_), channel_id=1, source_target_pairs={{1,0},{2,1},{3,2},{5,4},{6,5},{7,6},{9,8},{10,9},{11,10},{13,12},{... | collective-permute-start | bytes 2359304 | tf_op jit(solution)/shard_map/ppermute | solution.py:20
  32.8 4.6 %encode.4.refs_0_ = bf16[2,6,128,256]{3,2,1,0:T(8,128)(2,1)} custom-call(bf16[2,12,128,256]{3,2,1,0:T(8,128)(2,1)} %image_ref.6, bf16[2,2,12,256]{3,2,1,0:T(8,128)(2,1)} %copy-done, bf16[2,2,12,256]{3,2,1,0:T(8,128)(2,1)} %copy-done.1, bf16[2,2,130,256]{3,2,1,0:T(8,128)(2,1)} %copy-done.2, bf16[2,2,130,256]{3,2,1,0:T(8,128)(2,1)} %collective-permute-done.3.rest_1_, ...), custom_call_target="tpu_custom_call" | custom-call | flops 1811939328 | bytes 1572864 | tf_op jit(solution)/shard_map/encode/pallas_call | solution.py:99
  37.5 1.9 %collective-permute-start.5 = (bf16[2,6,128,256]{3,2,1,0:T(8,128)(2,1)}, bf16[2,6,128,256]{3,2,1,0:T(8,128)(2,1)}, u32[]{:S(2)}, u32[]{:S(2)}) collective-permute-start(bf16[2,6,128,256]{3,2,1,0:T(8,128)(2,1)} %encode.4.refs_0_), channel_id=1, source_target_pairs={{1,0},{2,1},{3,2},{5,4},{6,5},{7,6},{9,8},{10,9},{11,10},{13,12},{... | collective-permute-start | bytes 2359304 | tf_op jit(solution)/shard_map/ppermute | solution.py:20
  39.4 5.1 %encode.5.refs_1_ = bf16[2,6,128,256]{3,2,1,0:T(8,128)(2,1)} custom-call(bf16[2,12,128,256]{3,2,1,0:T(8,128)(2,1)} %image_ref.7, bf16[2,2,12,256]{3,2,1,0:T(8,128)(2,1)} %copy-done, bf16[2,2,12,256]{3,2,1,0:T(8,128)(2,1)} %copy-done.1, bf16[2,2,130,256]{3,2,1,0:T(8,128)(2,1)} %copy-done.2, bf16[2,2,130,256]{3,2,1,0:T(8,128)(2,1)} %collective-permute-done.3.rest_1_, ...), custom_call_target="tpu_custom_call" | custom-call | flops 1811939328 | bytes 1572864 | tf_op jit(solution)/shard_map/encode/pallas_call | solution.py:99
  44.5 3.6 %collective-permute-start.4 = (bf16[2,6,128,256]{3,2,1,0:T(8,128)(2,1)}, bf16[2,6,128,256]{3,2,1,0:T(8,128)(2,1)}, u32[]{:S(2)}, u32[]{:S(2)}) collective-permute-start(bf16[2,6,128,256]{3,2,1,0:T(8,128)(2,1)} %encode.5.refs_1_), channel_id=1, source_target_pairs={{0,1},{1,2},{2,3},{4,5},{5,6},{6,7},{8,9},{9,10},{10,11},{12,13},{... | collective-permute-start | bytes 2359304 | tf_op jit(solution)/shard_map/ppermute | solution.py:20
  48.2 3.4 %triangle.3 = f32[1,6,128,128]{3,2,1,0:T(8,128)} custom-call(bf16[2,6,128,256]{3,2,1,0:T(8,128)(2,1)} %collective-permute-done.8.left_ref, bf16[2,6,128,256]{3,2,1,0:T(8,128)(2,1)} %collective-permute-done.7.right_ref.refs_2_), custom_call_target="tpu_custom_call" | custom-call | flops 100663296 | bytes 1572864 | tf_op jit(solution)/shard_map/triangle/pallas_call | solution.py:131
  51.6 2.9 %collective-permute-start.9 = (f32[1,6,128,128]{3,2,1,0:T(8,128)}, f32[1,6,128,128]{3,2,1,0:T(8,128)}, u32[]{:S(2)}, u32[]{:S(2)}) collective-permute-start(f32[1,6,128,128]{3,2,1,0:T(8,128)} %triangle.3), channel_id=1, source_target_pairs={{0,1},{1,2},{2,3},{4,5},{5,6},{6,7},{8,9},{9,10},{10,11},{12,13},{... | collective-permute-start | bytes 1179656 | tf_op jit(solution)/shard_map/ppermute | solution.py:20
  54.5 2.9 %collective-permute-done.4.right_ref.refs_2_ = bf16[2,6,128,256]{3,2,1,0:T(8,128)(2,1)} collective-permute-done((bf16[2,6,128,256]{3,2,1,0:T(8,128)(2,1)}, bf16[2,6,128,256]{3,2,1,0:T(8,128)(2,1)}, u32[]{:S(2)}, u32[]{:S(2)}) %collective-permute-start.4) | collective-permute-done | bytes 786464 | tf_op jit(solution)/shard_map/ppermute | solution.py:20
  57.4 3.4 %triangle.2 = f32[1,6,128,128]{3,2,1,0:T(8,128)} custom-call(bf16[2,6,128,256]{3,2,1,0:T(8,128)(2,1)} %collective-permute-done.5.left_ref, bf16[2,6,128,256]{3,2,1,0:T(8,128)(2,1)} %collective-permute-done.4.right_ref.refs_2_), custom_call_target="tpu_custom_call" | custom-call | flops 100663296 | bytes 1572864 | tf_op jit(solution)/shard_map/triangle/pallas_call | solution.py:131
  60.8 4.4 %collective-permute-start.6 = (f32[1,6,128,128]{3,2,1,0:T(8,128)}, f32[1,6,128,128]{3,2,1,0:T(8,128)}, u32[]{:S(2)}, u32[]{:S(2)}) collective-permute-start(f32[1,6,128,128]{3,2,1,0:T(8,128)} %triangle.2), channel_id=1, source_target_pairs={{0,1},{1,2},{2,3},{4,5},{5,6},{6,7},{8,9},{9,10},{10,11},{12,13},{... | collective-permute-start | bytes 1179656 | tf_op jit(solution)/shard_map/ppermute | solution.py:20
  65.2 5.2 %volume.2.refs_5_ = f32[2,12,480,128]{3,2,1,0:T(8,128)} custom-call(bf16[2,6,128,256]{3,2,1,0:T(8,128)(2,1)} %encode.6.refs_0_, bf16[2,6,128,256]{3,2,1,0:T(8,128)(2,1)} %encode.7.refs_1_, bf16[2,6,128,256]{3,2,1,0:T(8,128)(2,1)} %collective-permute-done.7.right_ref.refs_2_, f32[1,6,128,128]{3,2,1,0:T(8,128)} %collective-permute-done.9.refs_3_, ...), custom_call_target="tpu_custom_call" | custom-call | flops 553648128 | bytes 5308416 | tf_op jit(solution)/shard_map/volume/pallas_call | solution.py:204
  70.4 5.2 %volume.3 = f32[2,12,480,128]{3,2,1,0:T(8,128)} custom-call(bf16[2,6,128,256]{3,2,1,0:T(8,128)(2,1)} %encode.4.refs_0_, bf16[2,6,128,256]{3,2,1,0:T(8,128)(2,1)} %encode.5.refs_1_, bf16[2,6,128,256]{3,2,1,0:T(8,128)(2,1)} %collective-permute-done.4.right_ref.refs_2_, ...), custom_call_target="tpu_custom_call", output_to_operand_aliasing={{}: (5, {})} | custom-call | flops 553648128 | bytes 5308416 | tf_op jit(solution)/shard_map/volume/pallas_call | solution.py:204
  (22 shorter events, 0.8 us)
Async XLA Ops:
  2.0 7.7 %collective-permute-start = (bf16[2,2,12,256]{3,2,1,0:T(8,128)(2,1)S(1)}, bf16[2,2,12,256]{3,2,1,0:T(8,128)(2,1)S(1)}, u32[]{:S(2)}, u32[]{:S(2)}) collective-permute-start(bf16[2,2,12,256]{3,2,1,0:T(8,128)(2,1)S(1)} %pad_maximum_fusion.2), channel_id=1, source_target_pairs={{0,1},{1,2},{2,3},{4,5},{5,6},{6,7},{8,9},{9,10},{10,11},{12,13},{... | collective-permute-start | bytes 73736 | tf_op jit(solution)/shard_map/ppermute | solution.py:20
  5.8 5.2 %collective-permute-start.1 = (bf16[2,2,12,256]{3,2,1,0:T(8,128)(2,1)S(1)}, bf16[2,2,12,256]{3,2,1,0:T(8,128)(2,1)S(1)}, u32[]{:S(2)}, u32[]{:S(2)}) collective-permute-start(bf16[2,2,12,256]{3,2,1,0:T(8,128)(2,1)S(1)} %pad_maximum_fusion.3), channel_id=1, source_target_pairs={{1,0},{2,1},{3,2},{5,4},{6,5},{7,6},{9,8},{10,9},{11,10},{13,12},{... | collective-permute-start | bytes 73736 | tf_op jit(solution)/shard_map/ppermute | solution.py:20
  9.7 7.6 %copy-start = (bf16[2,2,12,256]{3,2,1,0:T(8,128)(2,1)}, bf16[2,2,12,256]{3,2,1,0:T(8,128)(2,1)S(1)}, u32[]{:S(2)}) copy-start(bf16[2,2,12,256]{3,2,1,0:T(8,128)(2,1)S(1)} %collective-permute-done.before_ref) | copy-start | bytes 73732
  11.0 6.3 %copy-start.1 = (bf16[2,2,12,256]{3,2,1,0:T(8,128)(2,1)}, bf16[2,2,12,256]{3,2,1,0:T(8,128)(2,1)S(1)}, u32[]{:S(2)}) copy-start(bf16[2,2,12,256]{3,2,1,0:T(8,128)(2,1)S(1)} %collective-permute-done.1.after_ref) | copy-start | bytes 73732
  11.0 21.1 %collective-permute-start.2 = (bf16[2,2,130,256]{3,2,1,0:T(8,128)(2,1)S(1)}, bf16[2,2,130,256]{3,2,1,0:T(8,128)(2,1)S(1)}, u32[]{:S(2)}, u32[]{:S(2)}) collective-permute-start(bf16[2,2,130,256]{3,2,1,0:T(8,128)(2,1)S(1)} %pad_maximum_fusion), channel_id=1, source_target_pairs={{0,4},{4,8},{8,12},{12,16},{16,20},{20,24},{24,28},{1,5},{5,9},{9,... | collective-permute-start | bytes 798728 | tf_op jit(solution)/shard_map/ppermute | solution.py:20
  14.2 18.6 %collective-permute-start.3 = (bf16[2,2,130,256]{3,2,1,0:T(8,128)(2,1)S(1)}, bf16[2,2,130,256]{3,2,1,0:T(8,128)(2,1)}, u32[]{:S(2)}, u32[]{:S(2)}) collective-permute-start(bf16[2,2,130,256]{3,2,1,0:T(8,128)(2,1)S(1)} %pad_maximum_fusion.1), channel_id=1, source_target_pairs={{4,0},{8,4},{12,8},{16,12},{20,16},{24,20},{28,24},{5,1},{9,5},{13... | collective-permute-start | bytes 798728 | tf_op jit(solution)/shard_map/ppermute | solution.py:20
  22.4 25.8 %collective-permute-start.7 = (bf16[2,6,128,256]{3,2,1,0:T(8,128)(2,1)}, bf16[2,6,128,256]{3,2,1,0:T(8,128)(2,1)}, u32[]{:S(2)}, u32[]{:S(2)}) collective-permute-start(bf16[2,6,128,256]{3,2,1,0:T(8,128)(2,1)} %encode.7.refs_1_), channel_id=1, source_target_pairs={{0,1},{1,2},{2,3},{4,5},{5,6},{6,7},{8,9},{9,10},{10,11},{12,13},{... | collective-permute-start | bytes 2359304 | tf_op jit(solution)/shard_map/ppermute | solution.py:20
  29.9 18.3 %collective-permute-start.8 = (bf16[2,6,128,256]{3,2,1,0:T(8,128)(2,1)}, bf16[2,6,128,256]{3,2,1,0:T(8,128)(2,1)}, u32[]{:S(2)}, u32[]{:S(2)}) collective-permute-start(bf16[2,6,128,256]{3,2,1,0:T(8,128)(2,1)} %encode.6.refs_0_), channel_id=1, source_target_pairs={{1,0},{2,1},{3,2},{5,4},{6,5},{7,6},{9,8},{10,9},{11,10},{13,12},{... | collective-permute-start | bytes 2359304 | tf_op jit(solution)/shard_map/ppermute | solution.py:20
  32.1 0.7 copy-start.2
  37.5 17.1 %collective-permute-start.5 = (bf16[2,6,128,256]{3,2,1,0:T(8,128)(2,1)}, bf16[2,6,128,256]{3,2,1,0:T(8,128)(2,1)}, u32[]{:S(2)}, u32[]{:S(2)}) collective-permute-start(bf16[2,6,128,256]{3,2,1,0:T(8,128)(2,1)} %encode.4.refs_0_), channel_id=1, source_target_pairs={{1,0},{2,1},{3,2},{5,4},{6,5},{7,6},{9,8},{10,9},{11,10},{13,12},{... | collective-permute-start | bytes 2359304 | tf_op jit(solution)/shard_map/ppermute | solution.py:20
  44.5 12.9 %collective-permute-start.4 = (bf16[2,6,128,256]{3,2,1,0:T(8,128)(2,1)}, bf16[2,6,128,256]{3,2,1,0:T(8,128)(2,1)}, u32[]{:S(2)}, u32[]{:S(2)}) collective-permute-start(bf16[2,6,128,256]{3,2,1,0:T(8,128)(2,1)} %encode.5.refs_1_), channel_id=1, source_target_pairs={{0,1},{1,2},{2,3},{4,5},{5,6},{6,7},{8,9},{9,10},{10,11},{12,13},{... | collective-permute-start | bytes 2359304 | tf_op jit(solution)/shard_map/ppermute | solution.py:20
  51.6 13.6 %collective-permute-start.9 = (f32[1,6,128,128]{3,2,1,0:T(8,128)}, f32[1,6,128,128]{3,2,1,0:T(8,128)}, u32[]{:S(2)}, u32[]{:S(2)}) collective-permute-start(f32[1,6,128,128]{3,2,1,0:T(8,128)} %triangle.3), channel_id=1, source_target_pairs={{0,1},{1,2},{2,3},{4,5},{5,6},{6,7},{8,9},{9,10},{10,11},{12,13},{... | collective-permute-start | bytes 1179656 | tf_op jit(solution)/shard_map/ppermute | solution.py:20
  60.8 9.6 %collective-permute-start.6 = (f32[1,6,128,128]{3,2,1,0:T(8,128)}, f32[1,6,128,128]{3,2,1,0:T(8,128)}, u32[]{:S(2)}, u32[]{:S(2)}) collective-permute-start(f32[1,6,128,128]{3,2,1,0:T(8,128)} %triangle.2), channel_id=1, source_target_pairs={{0,1},{1,2},{2,3},{4,5},{5,6},{6,7},{8,9},{9,10},{10,11},{12,13},{... | collective-permute-start | bytes 1179656 | tf_op jit(solution)/shard_map/ppermute | solution.py:20
